TPU v7x, 32 devices: a whole 2x2x4 slice. The times are simulated.
32 devices in a mesh: seq: 8 (over z, x), head: 4 (over y, core).
Axes of the slice: x: 2, y: 2, z: 4, core: 2. Of those that a mesh axis runs over, the one named last changes fastest.
Arguments:
- tokens: bfloat16 [2048, 4608], P('seq', 'head'), may hold values from -32 to 32
- segments: int32 [2048], P('seq'), may hold values from 0 to 7, never falling along the last dimension, each value on 1 to 1024 neighbouring positions
- pre_gain: float32 [4608], replicated, may hold values from 0.1 to 1.9
- post_gain: float32 [4608], replicated, may hold values from 0.1 to 1.9
- w_query: bfloat16 [4608, 1024], P('seq', 'head'), may hold values from -0.375 to 0.375
- w_key: bfloat16 [4608, 512], P('seq', 'head'), may hold values from -0.1875 to 0.1875
- w_value: bfloat16 [4608, 512], P('seq', 'head'), may hold values from -0.09375 to 0.09375
- w_out: bfloat16 [1024, 4608], P('head', 'seq'), may hold values from -0.1875 to 0.1875
Outputs:
- mixed: bfloat16 [2048, 4608], P('seq')
Inputs may be any that keep to these rules, and one draw needn't show every extreme that they name: `segments`: segment ids never fall; each of the 8 documents holds at least one token and at most 1024, one exactly 1024.
All inputs are finite; a program needn't handle non-finite values.
Results may differ from a plain program's by a relative error of at most 0.01.
Values may be sent and summed in bfloat16 or wider, within the bound.
A program may use at most 64 MiB of HBM per device.

v0:
```python
import functools

import jax
import jax.numpy as jnp
import numpy as np
from jax import lax
from jax.experimental import pallas as pl
from jax.experimental.pallas import tpu as pltpu
from jax.sharding import PartitionSpec as P

HD = 128
GROUP = 2
SCALAR = 144
DOCS = 8


EPS = 1e-06
CAP = 50.0


def carried_in(value, axis, join, neutral):
    count, mine = (lax.axis_size(axis), lax.axis_index(axis))
    pieces = lax.all_gather(value, axis)
    subtotal = jnp.full_like(value, 0) + jnp.asarray(neutral, value.dtype)

    def step(position, subtotal):
        longer = join(subtotal, pieces[position])
        return jnp.where(position < mine, longer, subtotal)

    return lax.fori_loop(0, count - 1, step, subtotal)


def rotate(values, position, width):
    count = values.shape[1] // width
    half = width // 2
    shaped = values.reshape(values.shape[0], count, width)
    freq = 10000.0 ** (-(jnp.arange(half, dtype=jnp.float32) / half))
    angle = position[:, None] * freq[None, :]
    cosine = jnp.cos(angle)[:, None, :]
    sine = jnp.sin(angle)[:, None, :]
    first = shaped[:, :, :half]
    second = shaped[:, :, half:]
    turned = jnp.concatenate(
        [first * cosine - second * sine, second * cosine + first * sine], axis=2
    )
    return turned.reshape(values.shape[0], count * width)


def add_counts(earlier, later):
    return earlier + later


def local(tokens, segments, pre_gain, post_gain, w_query, w_key, w_value, w_out):
    rows = tokens.shape[0]
    whole = lax.all_gather(tokens, "head", axis=1, tiled=True)
    wide = whole.astype(jnp.float32)
    normed = (
        wide * lax.rsqrt(jnp.mean(wide * wide, axis=1, keepdims=True) + EPS) * pre_gain
    ).astype(jnp.bfloat16)
    pieces = (
        lax.all_gather(w_query, "seq", axis=0, tiled=True),
        lax.all_gather(w_key, "seq", axis=0, tiled=True),
        lax.all_gather(w_value, "seq", axis=0, tiled=True),
    )
    query, key_proj, value_proj = tuple(
        (jnp.dot(normed, piece, preferred_element_type=jnp.float32) for piece in pieces)
    )
    levels = jnp.arange(DOCS, dtype=jnp.int32)
    below = jnp.sum((levels[None, :] > segments[:, None]).astype(jnp.float32), axis=0)
    earlier = carried_in(below, "seq", add_counts, jnp.zeros((DOCS,), jnp.float32))
    starts = earlier + below
    onehot = (segments[:, None] == levels[None, :]).astype(jnp.float32)
    tok_start = jnp.sum(onehot * starts[None, :], axis=1)
    offset = lax.axis_index("seq") * rows
    index_f = (offset + jnp.arange(rows, dtype=jnp.int32)).astype(jnp.float32)
    position = index_f - tok_start
    kv_count = w_key.shape[1] // HD
    rq = (rotate(query, position, HD) * SCALAR ** (-0.5)).astype(jnp.bfloat16)
    rk = rotate(key_proj, position, HD).astype(jnp.bfloat16)
    vb = value_proj.astype(jnp.bfloat16)
    stacked = (
        rq.reshape(rows, kv_count, GROUP, HD)
        .transpose(1, 2, 0, 3)
        .reshape(kv_count, GROUP * rows, HD)
    )
    query_start = jnp.tile(tok_start, GROUP)
    query_index = jnp.tile(index_f, GROUP)
    empty = (
        jnp.zeros((kv_count, GROUP * rows, HD), jnp.float32),
        jnp.zeros((kv_count, GROUP * rows), jnp.float32),
    )
    keys_all = lax.all_gather(rk, "seq", axis=0, tiled=True)
    values_all = lax.all_gather(vb, "seq", axis=0, tiled=True)
    count = keys_all.shape[0]
    block = 1024
    steps_total = count // block

    def compute(offset_blk, state):
        numer, denom = state
        keys_blk = lax.dynamic_slice_in_dim(keys_all, offset_blk, block, 0).reshape(
            block, kv_count, HD
        )
        values_blk = lax.dynamic_slice_in_dim(values_all, offset_blk, block, 0).reshape(
            block, kv_count, HD
        )
        key_index = (offset_blk + jnp.arange(block, dtype=jnp.int32)).astype(jnp.float32)
        scores = jnp.einsum("cqd,kcd->cqk", stacked, keys_blk, preferred_element_type=jnp.float32)
        capped = CAP * jnp.tanh(scores / CAP)
        allowed = (key_index[None, None, :] >= query_start[None, :, None]) & (
            key_index[None, None, :] <= query_index[None, :, None]
        )
        weights = jnp.where(allowed, jnp.exp(capped), 0.0)
        numer = numer + jnp.einsum(
            "cqk,kcd->cqd",
            weights.astype(jnp.bfloat16),
            values_blk,
            preferred_element_type=jnp.float32,
        )
        denom = denom + jnp.sum(weights, axis=2)
        return (numer, denom)

    def one_block(step, state):
        offset_blk = step * block
        return compute(offset_blk, state)

    numer, denom = lax.fori_loop(0, steps_total, one_block, empty)
    attn = (numer / denom[:, :, None]).reshape(kv_count, GROUP, rows, HD).transpose(2, 0, 1, 3)
    attn = attn.reshape(rows, kv_count * GROUP * HD).astype(jnp.bfloat16)
    partial_proj = jnp.dot(
        attn, lax.all_gather(w_out, "seq", axis=1, tiled=True), preferred_element_type=jnp.float32
    )
    partial_proj = lax.optimization_barrier(partial_proj.astype(jnp.bfloat16)).astype(jnp.float32)
    summed = lax.psum(partial_proj.astype(jnp.bfloat16), "head").astype(jnp.float32)
    scale = lax.rsqrt(jnp.mean(summed * summed, axis=1, keepdims=True) + EPS)
    return (wide + summed * scale * post_gain).astype(jnp.bfloat16)


MESH = pl.DeviceIdType.MESH
BF16 = jnp.bfloat16
F32 = jnp.float32


def fits(mesh, tokens, w_key, w_out):
    seq, head = mesh.shape["seq"], mesh.shape["head"]
    width = tokens[1]
    weights = 2 * width * (w_key[1] // head) * (GROUP + 2)
    outs = 2 * w_out[0] * width
    rows = tokens[0] // seq
    rest = rows * width * (2 + 2 + 4 + 2) + tokens[0] * (w_key[1] // head) * 4
    return (
        seq % 2 == 0
        and seq > 2
        and head % 2 == 0
        and seq % (2 * head) == 0
        and w_key[1] // head == HD
        and (width // head) % 128 == 0
        and weights + outs + rest < 40 * 2**20
    )


class Line:
    def __init__(self, ref, recv, send, seq, down=True):
        self.ref, self.recv, self.send, self.down = ref, recv, send, down
        self.count = seq // 2
        me = lax.axis_index("seq")
        self.z, self.x = me // 2, lax.rem(me, 2)
        self.head = lax.axis_index("head")
        self.me = me

    def copy(self, block, way):
        target = (
            2 * (self.z + 1) + self.x,
            2 * (self.z - 1) + self.x,
            2 * self.z + 1 - self.x,
        )[way]
        return pltpu.make_async_remote_copy(
            src_ref=self.ref(block),
            dst_ref=self.ref(block),
            send_sem=self.send.at[way, block],
            recv_sem=self.recv.at[block],
            device_id=(target, self.head),
            device_id_type=MESH,
        )

    def up(self, block):
        @pl.when(self.z < self.count - 1)
        def _():
            self.copy(block, 0).start()

    def below(self, block):
        if self.down:

            @pl.when(self.z > 0)
            def _():
                self.copy(block, 1).start()

    def across(self, block):
        self.copy(block, 2).start()

    def wait(self, block):
        self.copy(block, 2).wait_recv()

    def at(self, k, act):
        @pl.when(self.z - k >= 0)
        def _():
            act(2 * (self.z - k) + self.x, self.up)

        if self.down:

            @pl.when(self.z + k < self.count)
            def _():
                act(2 * (self.z + k) + self.x, self.below)

    def near(self, k, also):
        def act(block, onward):
            self.wait(block)
            onward(block)
            also(block)

        self.at(k, act)

    def far(self, k):
        self.at(k, lambda block, onward: self.across(block))

    def step(self, k):
        self.near(k, self.across)

    def pairs(self, also=None, first=0, last=None):
        for away in range(first, self.count if last is None else last):
            z = lax.rem(self.z + away, self.count)
            block = 2 * z + 1 - self.x

            def take():
                self.wait(block)
                if also is not None:
                    also(block)

            if self.down:
                take()
            else:
                pl.when(z <= self.z)(take)

    def drain(self):
        for z in range(self.count):
            block = 2 * z + self.x

            def sent():
                self.copy(block, 2).wait_send()

            if self.down:
                sent()

                @pl.when((self.z > 0) & (z >= self.z))
                def _():
                    self.copy(block, 1).wait_send()
            else:
                pl.when(z <= self.z)(sent)

            @pl.when((self.z < self.count - 1) & (z <= self.z))
            def _():
                self.copy(block, 0).wait_send()


def kernel(
    seq, heads, rows, width,
    tok, seg_row, wq, wk, wv, wo_in, pre_in, post_in, freq_in,
    out,
    X, XN, W, WO, SEG, KV, ATT, PR, ACC, RQ, NUM, DEN, pre, post, freq,
    loc, x_recv, x_send, x_core, s_recv, s_send, w_recv, w_send,
    o_recv, o_send, o_y, o_core, k_recv, k_send, a_recv, a_send, a_core,
):
    me, head = lax.axis_index("seq"), lax.axis_index("head")
    z, x = me // 2, lax.rem(me, 2)
    y, core = head // 2, lax.rem(head, 2)
    ys, line = heads // 2, seq // 2
    partner = 2 * y + 1 - core
    deep = width // seq
    cut = width // heads
    mates = [2 * lax.rem(y + d, ys) + core for d in range(1, ys)]

    moves = [
        pltpu.make_async_copy(seg_row, SEG.at[me], loc.at[0]),
        pltpu.make_async_copy(tok, X.at[head], loc.at[1]),
    ]
    mine = W.at[pl.ds(pl.multiple_of(me * deep, 16), deep)]
    kd = wk.shape[1]
    qd = wq.shape[1]
    moves += [
        pltpu.make_async_copy(wq, mine.at[:, pl.ds(0, qd)], loc.at[2]),
        pltpu.make_async_copy(wk, mine.at[:, pl.ds(qd, kd)], loc.at[3]),
        pltpu.make_async_copy(wv, mine.at[:, pl.ds(qd + kd, kd)], loc.at[4]),
        pltpu.make_async_copy(
            wo_in, WO.at[head, pl.ds(pl.multiple_of(me * deep, 16), deep)], loc.at[5]
        ),
    ]
    small = [
        pltpu.make_async_copy(pre_in, pre, loc.at[6]),
        pltpu.make_async_copy(post_in, post, loc.at[7]),
        pltpu.make_async_copy(freq_in, freq, loc.at[8]),
    ]
    for move in small:
        move.start()
    for move in moves:
        move.start()

    barrier = pltpu.get_barrier_semaphore()

    def greet(where):
        pl.semaphore_signal(barrier, inc=1, device_id=where, device_id_type=MESH)

    greet((2 * z + 1 - x, head))
    greet((me, partner))
    for mate in mates:
        greet((me, mate))

    @pl.when(z > 0)
    def _():
        greet((me - 2, head))

    @pl.when(z < line - 1)
    def _():
        greet((me + 2, head))

    ends = (z > 0).astype(jnp.int32) + (z < line - 1).astype(jnp.int32)
    pl.semaphore_wait(barrier, 2 + len(mates) + ends)

    for move in moves:
        move.wait()

    def sent_to(ref, send, recv, where):
        return pltpu.make_async_remote_copy(
            src_ref=ref, dst_ref=ref, send_sem=send, recv_sem=recv,
            device_id=where, device_id_type=MESH,
        )

    def x_copy(h, to, send):
        return sent_to(X.at[h], send, x_recv.at[h], (me, to))

    def a_copy(h, to, send):
        return sent_to(ATT.at[h], send, a_recv.at[h], (me, to))

    def o_block(b, h):
        return WO.at[h, pl.ds(pl.multiple_of(b * deep, 16), deep)]

    def o_copy(b, h, to, send):
        return sent_to(o_block(b, h), send, o_recv.at[b, h], (me, to))

    segs = Line(lambda b: SEG.at[b], s_recv, s_send, seq)
    ws = Line(lambda b: W.at[pl.ds(pl.multiple_of(b * deep, 16), deep)], w_recv, w_send, seq)
    kvs = Line(lambda b: KV.at[b], k_recv, k_send, seq, down=False)
    wos = Line(lambda b: o_block(b, head), o_recv.at[:, head], o_send, seq)

    def share(b):
        for d, mate in enumerate(mates):
            o_copy(b, head, mate, o_y.at[d, b]).start()
        o_copy(b, head, partner, o_core.at[b, y]).start()

    def begin(stream):
        stream.up(me)
        stream.below(me)
        stream.across(me)

    begin(segs)
    for d, mate in enumerate(mates):
        x_copy(head, mate, x_send.at[d]).start()
    x_copy(head, partner, x_core.at[y]).start()
    begin(ws)
    share(me)

    def onset(k):
        @pl.when(z == k)
        def _():
            wos.up(me)

        @pl.when(line - 1 - z == k)
        def _():
            wos.below(me)

    onset(0)
    for move in small:
        move.wait()
    for mate in mates:
        x_copy(mate, partner, x_core.at[mate // 2]).wait_recv()
        x_copy(mate, partner, x_core.at[mate // 2]).start()
    segs.step(1)
    ws.step(1)
    onset(1)
    for other in range(ys):
        x_copy(2 * other + 1 - core, partner, x_core.at[other]).wait_recv()

    half = rows // 2

    def norm_rows(r, _):
        at = pl.ds(pl.multiple_of(r * half, half), half)
        total = jnp.zeros((half, 1), F32)
        for h in range(heads):
            wide = X[h, at, :].astype(F32)
            total += jnp.sum(wide * wide, axis=1, keepdims=True)
        scale = lax.rsqrt(total / width + EPS)
        for h in range(heads):
            gain = pre[0:1, h * cut : (h + 1) * cut]
            XN[h, at, :] = (X[h, at, :].astype(F32) * scale * gain).astype(BF16)
        return 0

    lax.fori_loop(0, 2, norm_rows, 0)
    for k in range(2, line):
        segs.step(k)
        ws.step(k)
        onset(k)
    wos.across(me)
    segs.pairs()
    own = jnp.broadcast_to(SEG[me].astype(F32), (HD, rows))
    col = jnp.transpose(own)[:, 0:1]
    start = jnp.zeros((rows, 1), F32)
    for j in range(seq):
        start += jnp.sum((SEG[j].astype(F32) < col).astype(F32), axis=1, keepdims=True)
    index = (me * rows + lax.broadcasted_iota(jnp.int32, (rows, 1), 0)).astype(F32)
    angle = (index - start) * freq[...]
    cosine = jnp.cos(angle)
    sine = jnp.sin(angle)
    lane = lax.broadcasted_iota(jnp.int32, (rows, HD), 1)
    sine = jnp.where(lane < HD // 2, -sine, sine)
    wos.near(1, share)
    ws.pairs()

    ACC[...] = jnp.zeros_like(ACC)

    def project(h, _):
        part = W[pl.ds(pl.multiple_of(h * cut, 128), cut), :]
        ACC[...] += jnp.dot(XN[h], part, preferred_element_type=F32)
        return 0

    lax.fori_loop(0, heads, project, 0)

    def turn(values):
        return values * cosine + pltpu.roll(values, HD // 2, 1) * sine

    for g in range(GROUP):
        RQ[g * rows : (g + 1) * rows, :] = (
            turn(ACC[:, g * HD : (g + 1) * HD]) * SCALAR ** (-0.5)
        ).astype(BF16)
    KV[me, :, 0:HD] = turn(ACC[:, qd : qd + HD]).astype(BF16)
    KV[me, :, HD : 2 * HD] = ACC[:, qd + kd : qd + kd + HD].astype(BF16)
    wos.far(1)
    begin(kvs)
    wos.pairs(share, 0, 1)
    for k in range(1, line):
        if k + 1 < line:
            wos.near(k + 1, share)
        kvs.step(k)
        if k > 1:
            wos.far(k)
    kvs.pairs()

    start2 = jnp.concatenate([start] * GROUP, axis=0)
    index2 = jnp.concatenate([index] * GROUP, axis=0)
    NUM[...] = jnp.zeros_like(NUM)
    DEN[...] = jnp.zeros_like(DEN)

    def attend(j, _):
        s = lax.dot_general(
            RQ[...], KV[j, :, 0:HD], (((1,), (1,)), ((), ())), preferred_element_type=F32
        )
        at = (j * rows + lax.broadcasted_iota(jnp.int32, (1, rows), 1)).astype(F32)
        p = jnp.where(
            (at >= start2) & (at <= index2), jnp.exp(CAP * jnp.tanh(s * (1.0 / CAP))), 0.0
        )
        DEN[...] += jnp.sum(p, axis=1, keepdims=True)
        NUM[...] += jnp.dot(p.astype(BF16), KV[j, :, HD : 2 * HD], preferred_element_type=F32)
        return 0

    lax.fori_loop(0, me + 1, attend, 0)
    ratio = (NUM[...] / DEN[:, 0:1]).astype(BF16)
    for g in range(GROUP):
        ATT[head, :, g * HD : (g + 1) * HD] = ratio[g * rows : (g + 1) * rows, :]
    for d, mate in enumerate(mates):
        a_copy(head, mate, a_send.at[d]).start()
    a_copy(head, partner, a_core.at[y]).start()

    group = line // heads
    nest = z // group
    less = jnp.minimum(nest, heads - 1 - nest)
    low = (nest <= heads - 1 - nest).astype(jnp.int32)

    def nearest(i):
        near = (i <= 2 * less).astype(jnp.int32)
        beside = nest + ((i + 1) // 2) * (1 - 2 * (i % 2))
        past = low * i + (1 - low) * (heads - 1 - i)
        return near * beside + (1 - near) * past

    for i in range(heads):
        for t in range(group):
            there = nearest(i) * group + t
            block = 2 * there + 1 - x

            @pl.when(there != z)
            def _():
                wos.wait(block)
                share(block)

    for mate in mates:
        a_copy(mate, partner, a_core.at[mate // 2]).wait_recv()
        a_copy(mate, partner, a_core.at[mate // 2]).start()
    for other in range(ys):
        a_copy(2 * other + 1 - core, partner, a_core.at[other]).wait_recv()

    total = jnp.zeros((rows, 1), F32)
    for i in range(heads):
        n = nearest(i)
        for j in range(2 * group):
            b = 2 * n * group + j
            for mate in mates:
                o_copy(b, mate, partner, o_core.at[b, mate // 2]).wait_recv()
                o_copy(b, mate, partner, o_core.at[b, mate // 2]).start()
        for j in range(2 * group):
            b = 2 * n * group + j
            for other in range(ys):
                o_copy(b, 2 * other + 1 - core, partner, o_core.at[b, other]).wait_recv()
        at = pl.ds(pl.multiple_of(n * cut, 128), cut)

        def emit(r, _):
            some = pl.ds(pl.multiple_of(r * half, half), half)
            acc = jnp.zeros((half, cut), F32)
            for h in range(heads):
                part = lax.dot_general(
                    ATT[h, some, :], WO[h, at, :], (((1,), (1,)), ((), ())),
                    preferred_element_type=F32,
                )
                acc += part.astype(BF16).astype(F32)
            PR[n, some, :] = acc
            return 0

        lax.fori_loop(0, 2, emit, 0)
        total += jnp.sum(PR[n] * PR[n], axis=1, keepdims=True)
    scale = lax.rsqrt(total / width + EPS)

    def finish(h, _):
        at = pl.ds(pl.multiple_of(h * cut, 128), cut)
        out[:, at] = (X[h].astype(F32) + PR[h] * scale * post[0:1, at]).astype(BF16)
        return 0

    lax.fori_loop(0, heads, finish, 0)

    for stream in (segs, ws, kvs, wos):
        stream.drain()
    for d, mate in enumerate(mates):
        x_copy(head, mate, x_send.at[d]).wait_send()
        a_copy(head, mate, a_send.at[d]).wait_send()
    for other in range(ys):
        x_copy(2 * other + core, partner, x_core.at[other]).wait_send()
        a_copy(2 * other + core, partner, a_core.at[other]).wait_send()
    for b in range(seq):
        for d, mate in enumerate(mates):
            o_copy(b, head, mate, o_y.at[d, b]).wait_send()
        for other in range(ys):
            o_copy(b, 2 * other + core, partner, o_core.at[b, other]).wait_send()


def fused(tokens, segments, pre_gain, post_gain, w_query, w_key, w_value, w_out):
    seq, heads = lax.axis_size("seq"), lax.axis_size("head")
    rows, cut = tokens.shape
    width = cut * heads
    deep = width // seq
    qd, kd = w_query.shape[1], w_key.shape[1]
    half = HD // 2
    freq = np.float32(10000.0) ** (-(np.arange(half, dtype=np.float32) / np.float32(half)))
    freq = np.concatenate([freq, freq])[None, :].astype(np.float32)
    hbm = pl.BlockSpec(memory_space=pl.ANY)
    vmem = pl.BlockSpec(memory_space=pltpu.VMEM)
    dma = pltpu.SemaphoreType.DMA
    ys = heads // 2
    return pl.pallas_call(
        functools.partial(kernel, seq, heads, rows, width),
        out_shape=jax.ShapeDtypeStruct((rows, width), BF16),
        in_specs=[hbm] * 9,
        out_specs=vmem,
        scratch_shapes=[
            pltpu.VMEM((heads, rows, cut), BF16),
            pltpu.VMEM((heads, rows, cut), BF16),
            pltpu.VMEM((width, qd + 2 * kd), BF16),
            pltpu.VMEM((heads, width, w_out.shape[0]), BF16),
            pltpu.VMEM((seq, 1, rows), jnp.int32),
            pltpu.VMEM((seq, rows, 2 * HD), BF16),
            pltpu.VMEM((heads, rows, GROUP * HD), BF16),
            pltpu.VMEM((heads, rows, cut), F32),
            pltpu.VMEM((rows, qd + 2 * kd), F32),
            pltpu.VMEM((GROUP * rows, HD), BF16),
            pltpu.VMEM((GROUP * rows, HD), F32),
            pltpu.VMEM((GROUP * rows, HD), F32),
            pltpu.VMEM((1, width), F32),
            pltpu.VMEM((1, width), F32),
            pltpu.VMEM((1, HD), F32),
            dma((9,)),
            dma((heads,)), dma((max(ys - 1, 1),)), dma((ys,)),
            dma((seq,)), dma((3, seq)),
            dma((seq,)), dma((3, seq)),
            dma((seq, heads)), dma((3, seq)), dma((max(ys - 1, 1), seq)), dma((seq, ys)),
            dma((seq,)), dma((3, seq)),
            dma((heads,)), dma((max(ys - 1, 1),)), dma((ys,)),
        ],
        compiler_params=pltpu.CompilerParams(
            collective_id=0, has_side_effects=True, vmem_limit_bytes=60 * 2**20
        ),
    )(
        tokens, segments[None, :], w_query, w_key, w_value, w_out.T,
        pre_gain[None, :], post_gain[None, :], freq,
    )


def solution(mesh):
    specs = (
        P("seq", "head"),
        P("seq"),
        P(),
        P(),
        P("seq", "head"),
        P("seq", "head"),
        P("seq", "head"),
        P("head", "seq"),
    )

    def run(*args):
        small = fits(mesh, args[0].shape, args[5].shape, args[7].shape)
        return jax.shard_map(
            fused if small else local,
            mesh=mesh,
            in_specs=specs,
            out_specs=P("seq", None),
            check_vma=False,
        )(*args)

    return run
```

profile of v0, /device:TPU:29, one launch (start us, length us, event | category | flops | bytes accessed | tf_op | source)
XLA Modules:
  0.0 122.9 jit_solution(15767042506244160402)
XLA Ops:
  0.0 1.3 %broadcast_in_dim.10.pre_in = f32[1,4608]{1,0:T(1,128)} reshape(f32[4608]{0:T(1024)} %param.11) | data formatting | bytes 36864 | tf_op jit(solution)/shard_map/broadcast_in_dim | solution.py:606
  1.3 1.3 %broadcast_in_dim.11.post_in = f32[1,4608]{1,0:T(1,128)} reshape(f32[4608]{0:T(1024)} %param.12) | data formatting | bytes 36864 | tf_op jit(solution)/shard_map/broadcast_in_dim | solution.py:606
  2.7 117.0 %shard_map.91 = bf16[256,4608]{1,0:T(8,128)(2,1)} custom-call(bf16[256,1152]{1,0:T(8,128)(2,1)} %tok.1, s32[1,256]{1,0:T(1,128)} %bitcast.3, bf16[576,256]{1,0:T(8,128)(2,1)} %wq.1, bf16[576,128]{1,0:T(8,128)(2,1)} %wk.1, bf16[576,128]{1,0:T(8,128)(2,1)} %wv.1, bf16[576,256]{1,0:T(8,128)(2,1)} %bitcast.2, f32[1,4608]{1,0:T(1,128)} %broadcast_in_dim.10.pre_in, ...), custom_call_target="tpu_custom_call" | custom-call | tf_op jit(solution)/shard_map/pallas_call | solution.py:572
  119.7 3.2 %copy.11 = bf16[256,4608]{1,0:T(8,128)(2,1)} copy(bf16[256,4608]{1,0:T(8,128)(2,1)} %shard_map.91) | data formatting | bytes 4718592
where the time goes:
time: 123 us
  Pallas kernels  117 us (95%)
  local copies, waits for them, and re-layouts  5.9 us (5%)
    pallas_call x1, Pallas kernels, fused(): pl.pallas_call(functools.partial(kernel, seq, heads, rows, width), out_sh...  117 us
    unnamed x1, local copies, waits for them, and re-layouts  3.22 us

commit v1 on v0

v1 whole, which is shorter than its diff:
```python
import functools

import jax
import jax.numpy as jnp
import numpy as np
from jax import lax
from jax.experimental import pallas as pl
from jax.experimental.pallas import tpu as pltpu
from jax.sharding import PartitionSpec as P

HD = 128
GROUP = 2
SCALAR = 144
DOCS = 8


EPS = 1e-06
CAP = 50.0


def carried_in(value, axis, join, neutral):
    count, mine = (lax.axis_size(axis), lax.axis_index(axis))
    pieces = lax.all_gather(value, axis)
    subtotal = jnp.full_like(value, 0) + jnp.asarray(neutral, value.dtype)

    def step(position, subtotal):
        longer = join(subtotal, pieces[position])
        return jnp.where(position < mine, longer, subtotal)

    return lax.fori_loop(0, count - 1, step, subtotal)


def rotate(values, position, width):
    count = values.shape[1] // width
    half = width // 2
    shaped = values.reshape(values.shape[0], count, width)
    freq = 10000.0 ** (-(jnp.arange(half, dtype=jnp.float32) / half))
    angle = position[:, None] * freq[None, :]
    cosine = jnp.cos(angle)[:, None, :]
    sine = jnp.sin(angle)[:, None, :]
    first = shaped[:, :, :half]
    second = shaped[:, :, half:]
    turned = jnp.concatenate(
        [first * cosine - second * sine, second * cosine + first * sine], axis=2
    )
    return turned.reshape(values.shape[0], count * width)


def add_counts(earlier, later):
    return earlier + later


def local(tokens, segments, pre_gain, post_gain, w_query, w_key, w_value, w_out):
    rows = tokens.shape[0]
    whole = lax.all_gather(tokens, "head", axis=1, tiled=True)
    wide = whole.astype(jnp.float32)
    normed = (
        wide * lax.rsqrt(jnp.mean(wide * wide, axis=1, keepdims=True) + EPS) * pre_gain
    ).astype(jnp.bfloat16)
    pieces = (
        lax.all_gather(w_query, "seq", axis=0, tiled=True),
        lax.all_gather(w_key, "seq", axis=0, tiled=True),
        lax.all_gather(w_value, "seq", axis=0, tiled=True),
    )
    query, key_proj, value_proj = tuple(
        (jnp.dot(normed, piece, preferred_element_type=jnp.float32) for piece in pieces)
    )
    levels = jnp.arange(DOCS, dtype=jnp.int32)
    below = jnp.sum((levels[None, :] > segments[:, None]).astype(jnp.float32), axis=0)
    earlier = carried_in(below, "seq", add_counts, jnp.zeros((DOCS,), jnp.float32))
    starts = earlier + below
    onehot = (segments[:, None] == levels[None, :]).astype(jnp.float32)
    tok_start = jnp.sum(onehot * starts[None, :], axis=1)
    offset = lax.axis_index("seq") * rows
    index_f = (offset + jnp.arange(rows, dtype=jnp.int32)).astype(jnp.float32)
    position = index_f - tok_start
    kv_count = w_key.shape[1] // HD
    rq = (rotate(query, position, HD) * SCALAR ** (-0.5)).astype(jnp.bfloat16)
    rk = rotate(key_proj, position, HD).astype(jnp.bfloat16)
    vb = value_proj.astype(jnp.bfloat16)
    stacked = (
        rq.reshape(rows, kv_count, GROUP, HD)
        .transpose(1, 2, 0, 3)
        .reshape(kv_count, GROUP * rows, HD)
    )
    query_start = jnp.tile(tok_start, GROUP)
    query_index = jnp.tile(index_f, GROUP)
    empty = (
        jnp.zeros((kv_count, GROUP * rows, HD), jnp.float32),
        jnp.zeros((kv_count, GROUP * rows), jnp.float32),
    )
    keys_all = lax.all_gather(rk, "seq", axis=0, tiled=True)
    values_all = lax.all_gather(vb, "seq", axis=0, tiled=True)
    count = keys_all.shape[0]
    block = 1024
    steps_total = count // block

    def compute(offset_blk, state):
        numer, denom = state
        keys_blk = lax.dynamic_slice_in_dim(keys_all, offset_blk, block, 0).reshape(
            block, kv_count, HD
        )
        values_blk = lax.dynamic_slice_in_dim(values_all, offset_blk, block, 0).reshape(
            block, kv_count, HD
        )
        key_index = (offset_blk + jnp.arange(block, dtype=jnp.int32)).astype(jnp.float32)
        scores = jnp.einsum("cqd,kcd->cqk", stacked, keys_blk, preferred_element_type=jnp.float32)
        capped = CAP * jnp.tanh(scores / CAP)
        allowed = (key_index[None, None, :] >= query_start[None, :, None]) & (
            key_index[None, None, :] <= query_index[None, :, None]
        )
        weights = jnp.where(allowed, jnp.exp(capped), 0.0)
        numer = numer + jnp.einsum(
            "cqk,kcd->cqd",
            weights.astype(jnp.bfloat16),
            values_blk,
            preferred_element_type=jnp.float32,
        )
        denom = denom + jnp.sum(weights, axis=2)
        return (numer, denom)

    def one_block(step, state):
        offset_blk = step * block
        return compute(offset_blk, state)

    numer, denom = lax.fori_loop(0, steps_total, one_block, empty)
    attn = (numer / denom[:, :, None]).reshape(kv_count, GROUP, rows, HD).transpose(2, 0, 1, 3)
    attn = attn.reshape(rows, kv_count * GROUP * HD).astype(jnp.bfloat16)
    partial_proj = jnp.dot(
        attn, lax.all_gather(w_out, "seq", axis=1, tiled=True), preferred_element_type=jnp.float32
    )
    partial_proj = lax.optimization_barrier(partial_proj.astype(jnp.bfloat16)).astype(jnp.float32)
    summed = lax.psum(partial_proj.astype(jnp.bfloat16), "head").astype(jnp.float32)
    scale = lax.rsqrt(jnp.mean(summed * summed, axis=1, keepdims=True) + EPS)
    return (wide + summed * scale * post_gain).astype(jnp.bfloat16)


MESH = pl.DeviceIdType.MESH
BF16 = jnp.bfloat16
F32 = jnp.float32


def fits(mesh, tokens, w_key, w_out):
    seq, head = mesh.shape["seq"], mesh.shape["head"]
    width = tokens[1]
    weights = 2 * width * (w_key[1] // head) * (GROUP + 2)
    outs = 2 * w_out[0] * width
    rows = tokens[0] // seq
    rest = rows * width * (4 + 2 + 4 + 2) + tokens[0] * (w_key[1] // head) * 4
    return (
        head == 4
        and seq == 2 * head
        and w_key[1] // head == HD
        and (width // head) % 128 == 0
        and weights + outs + rest < 44 * 2**20
    )


class Line:
    def __init__(self, ref, recv, send, seq, lane, across, reach=None):
        self.ref, self.recv, self.send = ref, recv, send
        self.count = seq // 2
        self.me = lax.axis_index("seq")
        self.head = lax.axis_index("head")
        self.z = self.me // 2
        self.lane, self.side = lane, across
        self.reach = reach

    def copy(self, zz, way):
        block = 2 * zz + self.lane
        target = ((self.me + 2, self.head), (self.me - 2, self.head), self.side)[way]
        return pltpu.make_async_remote_copy(
            src_ref=self.ref(block),
            dst_ref=self.ref(block),
            send_sem=self.send.at[way, zz],
            recv_sem=self.recv.at[block],
            device_id=target,
            device_id_type=MESH,
        )

    def rises(self, zz):
        if self.reach is None:
            return (zz <= self.z) & (self.z < self.count - 1)
        return (zz <= self.z) & (self.z < self.count - 1) & (self.z - zz < self.reach)

    def sinks(self, zz):
        return (zz >= self.z) & (self.z > 0)

    def held(self, zz):
        return (zz <= self.z) & (self.z - zz <= self.reach)

    def begin(self):
        self.onward(self.z)
        self.across(self.z)

    def onward(self, zz):
        @pl.when(self.rises(zz))
        def _():
            self.copy(zz, 0).start()

        if self.reach is None:

            @pl.when(self.sinks(zz))
            def _():
                self.copy(zz, 1).start()

    def across(self, zz):
        self.copy(zz, 2).start()

    def take(self, zz):
        self.copy(zz, 2).wait_recv()

    def near(self, k):
        def act(zz):
            self.take(zz)
            self.onward(zz)
            self.across(zz)

        @pl.when(self.z >= k)
        def _():
            act(self.z - k)

        if self.reach is None:

            @pl.when(self.z + k < self.count)
            def _():
                act(self.z + k)

    def beside(self, zz):
        pltpu.make_async_remote_copy(
            src_ref=self.ref(2 * zz + 1 - self.lane),
            dst_ref=self.ref(2 * zz + 1 - self.lane),
            send_sem=self.send.at[2, zz],
            recv_sem=self.recv.at[2 * zz + 1 - self.lane],
            device_id=self.side,
            device_id_type=MESH,
        ).wait_recv()

    def pairs(self):
        for zz in range(self.count):
            if self.reach is None:
                self.beside(zz)
            else:
                pl.when(self.held(zz))(functools.partial(self.beside, zz))

    def drain(self):
        for zz in range(self.count):
            for way, told in ((0, self.rises(zz)), (1, self.sinks(zz))):
                if way == 0 or self.reach is None:
                    pl.when(told)(functools.partial(self.sent, zz, way))
            if self.reach is None:
                self.sent(zz, 2)
            else:
                pl.when(self.held(zz))(functools.partial(self.sent, zz, 2))

    def sent(self, zz, way):
        self.copy(zz, way).wait_send()


def kernel(
    seq, heads, rows, width, most,
    tok, seg_row, wq, wk, wv, wo_in, pre_in, post_in, freq_in,
    out,
    TOK, X, XN, SW, W, WO, SEG, KV, AO, ATT, PR, ACC, RQ, NUM, DEN, pre, post, freq,
    loc, x_recv, x_send, r_recv, r_send, s_recv, s_send, w_recv, w_send, w_swap,
    o_recv, o_z, o_x, o_y, o_c, k_recv, k_send, a_recv, a_send, a_core,
):
    me, head = lax.axis_index("seq"), lax.axis_index("head")
    z, x = me // 2, lax.rem(me, 2)
    y, c = head // 2, lax.rem(head, 2)
    line = seq // 2
    deep = width // seq
    cut = width // heads
    qd, kd = wq.shape[1], wk.shape[1]
    same = c == x
    other = c != x
    partner = (me, 2 * y + 1 - c)
    xn = (2 * z + 1 - x, head)
    yhead = 2 * (1 - y) + c
    yn = (me, yhead)
    rb = 2 * z + c
    hg = 2 * y + x

    def wide_block(ref, b):
        return ref.at[pl.ds(pl.multiple_of(b * deep, 16), deep)]

    def remote(src, dst, send, recv, where):
        return pltpu.make_async_remote_copy(
            src_ref=src, dst_ref=dst, send_sem=send, recv_sem=recv,
            device_id=where, device_id_type=MESH,
        )

    def o_ref(b, h):
        return WO.at[h, pl.ds(pl.multiple_of(b * deep, 16), deep)]

    l_tok = pltpu.make_async_copy(tok, TOK, loc.at[0])
    l_own = pltpu.make_async_copy(tok, X.at[0, head], loc.at[1])
    l_seg = pltpu.make_async_copy(seg_row, SEG.at[me], loc.at[2])
    l_out = pltpu.make_async_copy(wo_in, o_ref(me, head), loc.at[3])

    def w_loads(block):
        return [
            pltpu.make_async_copy(wq, block.at[:, pl.ds(0, qd)], loc.at[4]),
            pltpu.make_async_copy(wk, block.at[:, pl.ds(qd, kd)], loc.at[5]),
            pltpu.make_async_copy(wv, block.at[:, pl.ds(qd + kd, kd)], loc.at[6]),
        ]

    small = [
        pltpu.make_async_copy(pre_in, pre, loc.at[7]),
        pltpu.make_async_copy(post_in, post, loc.at[8]),
        pltpu.make_async_copy(freq_in, freq, loc.at[9]),
    ]

    @pl.when(same)
    def _():
        for move in w_loads(wide_block(W, me)):
            move.start()

    @pl.when(other)
    def _():
        for move in w_loads(SW):
            move.start()

    l_tok.start()

    @pl.when(same)
    def _():
        l_own.start()

    l_seg.start()
    l_out.start()
    for move in small:
        move.start()

    barrier = pltpu.get_barrier_semaphore()

    def greet(where):
        pl.semaphore_signal(barrier, inc=1, device_id=where, device_id_type=MESH)

    for dx in range(2):
        for dy in range(2):
            for dc in range(2):
                if dx + dy + dc > 0:
                    gx = lax.rem(x + dx, 2)
                    greet((2 * z + gx, 2 * lax.rem(y + dy, 2) + lax.rem(c + dc, 2)))

    @pl.when(z > 0)
    def _():
        greet((me - 2, head))

    @pl.when(z < line - 1)
    def _():
        greet((me + 2, head))

    ends = (z > 0).astype(jnp.int32) + (z < line - 1).astype(jnp.int32)
    pl.semaphore_wait(barrier, 7 + ends)

    segs = Line(lambda b: SEG.at[b], s_recv, s_send, seq, x, xn)
    ws = Line(lambda b: wide_block(W, b), w_recv, w_send, seq, c, partner)
    kvs = Line(lambda b: KV.at[b], k_recv, k_send, seq, c, partner, most // (2 * rows))

    swap = remote(SW, wide_block(W, me), w_swap.at[0], w_recv.at[me], (2 * z + c, hg))

    def t_copy(i):
        where = (
            (me, 2 * y + x),
            (me, 2 * (1 - y) + x),
            (2 * z + 1 - x, 2 * y + x),
            (2 * z + 1 - x, 2 * (1 - y) + x),
        )[i]
        return remote(TOK, X.at[0, head], x_send.at[i], x_recv.at[head], where)

    def o_copy(way, zz, rel):
        fx, fy = rel
        b = 2 * zz + (1 - x if fx else x)
        h = yhead if fy else head
        send, where = {
            "up": (o_z.at[0, zz], (me + 2, head)),
            "down": (o_z.at[1, zz], (me - 2, head)),
            "x": (o_x.at[fy, zz], xn),
            "y": (o_y.at[fx, zz], yn),
            "c": (o_c.at[2 * fx + fy, zz], partner),
        }[way]
        return remote(o_ref(b, h), o_ref(b, h), send, o_recv.at[b, h], where)

    def o_z_onward(zz):
        @pl.when((zz <= z) & (z < line - 1))
        def _():
            o_copy("up", zz, (0, 0)).start()

        @pl.when((zz >= z) & (z > 0))
        def _():
            o_copy("down", zz, (0, 0)).start()

    def o_share(zz):
        o_copy("x", zz, (0, 0)).start()
        o_copy("y", zz, (0, 0)).start()
        o_copy("c", zz, (0, 0)).start()

    def o_take(zz, rel):
        o_copy("c", zz, rel).wait_recv()

    def both(k, act):
        if k == 0:
            act(z)
        else:

            @pl.when(z >= k)
            def _():
                act(z - k)

            @pl.when(z + k < line)
            def _():
                act(z + k)

    def o_from_z(zz):
        o_take(zz, (0, 0))
        o_z_onward(zz)
        o_share(zz)

    def o_from_x(zz):
        o_take(zz, (1, 0))

        @pl.when(lax.rem(zz, 2) == 1)
        def _():
            o_copy("y", zz, (1, 0)).start()

        o_copy("c", zz, (1, 0)).start()

    def o_from_y(zz):
        o_take(zz, (0, 1))

        @pl.when(lax.rem(zz, 2) == 0)
        def _():
            o_copy("x", zz, (0, 1)).start()

        o_copy("c", zz, (0, 1)).start()

    def o_from_d(zz):
        o_take(zz, (1, 1))
        o_copy("c", zz, (1, 1)).start()

    def o_from_c(zz):
        for bx in range(2):
            for hy in range(2):
                b, h = 2 * zz + bx, 2 * hy + 1 - c
                remote(o_ref(b, h), o_ref(b, h), o_c.at[0, zz], o_recv.at[b, h], partner).wait_recv()

    @pl.when(same)
    def _():
        for move in w_loads(wide_block(W, me)):
            move.wait()
        ws.begin()

    @pl.when(other)
    def _():
        for move in w_loads(SW):
            move.wait()
        swap.start()

    l_seg.wait()
    segs.begin()
    l_tok.wait()
    t_copy(1).start()

    @pl.when(other)
    def _():
        t_copy(0).start()
        t_copy(2).start()
        t_copy(3).start()
        ws.take(z)
        ws.begin()

    l_out.wait()
    o_z_onward(z)
    ws.near(1)

    @pl.when(same)
    def _():
        t_copy(2).start()
        t_copy(3).start()

    o_share(z)
    for k in range(1, line):
        segs.near(k)
    segs.pairs()
    for move in small:
        move.wait()

    own = jnp.broadcast_to(SEG[rb].astype(F32), (HD, rows))
    col = jnp.transpose(own)[:, 0:1]
    start = jnp.zeros((rows, 1), F32)
    for j in range(seq):
        start += jnp.sum((SEG[j].astype(F32) < col).astype(F32), axis=1, keepdims=True)
    index = (rb * rows + lax.broadcasted_iota(jnp.int32, (rows, 1), 0)).astype(F32)
    angle = (index - start) * freq[...]
    cosine = jnp.cos(angle)
    sine = jnp.sin(angle)
    lane = lax.broadcasted_iota(jnp.int32, (rows, HD), 1)
    sine = jnp.where(lane < HD // 2, -sine, sine)

    ws.near(2)
    both(1, o_from_z)

    def x_take(h):
        remote(TOK, X.at[0, h], x_send.at[0], x_recv.at[h], partner).wait_recv()

    def r_copy(h):
        return remote(X.at[0, h], X.at[1, h], r_send.at[h], r_recv.at[h], partner)

    for h in range(heads):
        @pl.when(same & (head == h))
        def _():
            l_own.wait()

        @pl.when(other | (head != h))
        def _():
            x_take(h)

        @pl.when(same)
        def _():
            r_copy(h).start()

    half = rows // 2

    def norm_rows(r, _):
        at = pl.ds(pl.multiple_of(r * half, half), half)
        total = jnp.zeros((half, 1), F32)
        for h in range(heads):
            wide = X[0, h, at, :].astype(F32)
            total += jnp.sum(wide * wide, axis=1, keepdims=True)
        scale = lax.rsqrt(total / width + EPS)
        for h in range(heads):
            gain = pre[h * cut : (h + 1) * cut][None, :]
            XN[h, at, :] = (X[0, h, at, :].astype(F32) * scale * gain).astype(BF16)
        return 0

    lax.fori_loop(0, 2, norm_rows, 0)
    o_from_x(z)
    o_from_y(z)
    o_from_d(z)
    for k in range(3, line):
        ws.near(k)
    ws.pairs()

    ACC[...] = jnp.zeros_like(ACC)

    def project(h, _):
        part = W[pl.ds(pl.multiple_of(h * cut, 128), cut), :]
        ACC[...] += jnp.dot(XN[h], part, preferred_element_type=F32)
        return 0

    lax.fori_loop(0, heads, project, 0)

    def turn(values):
        return values * cosine + pltpu.roll(values, HD // 2, 1) * sine

    KV[rb, :, 0:HD] = turn(ACC[:, qd : qd + HD]).astype(BF16)
    KV[rb, :, HD : 2 * HD] = ACC[:, qd + kd : qd + kd + HD].astype(BF16)
    kvs.begin()
    for g in range(GROUP):
        RQ[g * rows : (g + 1) * rows, :] = (
            turn(ACC[:, g * HD : (g + 1) * HD]) * SCALAR ** (-0.5)
        ).astype(BF16)

    both(1, o_from_x)
    both(1, o_from_y)
    both(1, o_from_d)
    kvs.near(1)
    both(2, o_from_z)
    for k in range(2, kvs.reach + 1):
        kvs.near(k)
    kvs.pairs()

    start2 = jnp.concatenate([start] * GROUP, axis=0)
    index2 = jnp.concatenate([index] * GROUP, axis=0)
    NUM[...] = jnp.zeros_like(NUM)
    DEN[...] = jnp.zeros_like(DEN)

    def attend(j, _):
        s = lax.dot_general(
            RQ[...], KV[j, :, 0:HD], (((1,), (1,)), ((), ())), preferred_element_type=F32
        )
        at = (j * rows + lax.broadcasted_iota(jnp.int32, (1, rows), 1)).astype(F32)
        p = jnp.where(
            (at >= start2) & (at <= index2), jnp.exp(CAP * jnp.tanh(s * (1.0 / CAP))), 0.0
        )
        DEN[...] += jnp.sum(p, axis=1, keepdims=True)
        NUM[...] += jnp.dot(p.astype(BF16), KV[j, :, HD : 2 * HD], preferred_element_type=F32)
        return 0

    lax.fori_loop(jnp.maximum(rb - most // rows, 0), rb + 1, attend, 0)
    ratio = (NUM[...] / DEN[:, 0:1]).astype(BF16)
    for g in range(GROUP):
        AO[:, g * HD : (g + 1) * HD] = ratio[g * rows : (g + 1) * rows, :]

    def a_copy(i):
        where = (
            (me, 2 * y + 1 - c),
            (me, yhead),
            (2 * z + 1 - x, head),
            (2 * z + 1 - x, yhead),
        )[i]
        return remote(AO, ATT.at[hg], a_send.at[i], a_recv.at[hg], where)

    def a_pass(h):
        return remote(ATT.at[h], ATT.at[h], a_core.at[h], a_recv.at[h], partner)

    @pl.when(same)
    def _():
        a_copy(1).start()
        a_copy(0).start()
        for g in range(GROUP):
            ATT[hg, :, g * HD : (g + 1) * HD] = ratio[g * rows : (g + 1) * rows, :]

    @pl.when(other)
    def _():
        a_copy(2).start()
        a_copy(3).start()

    both(2, o_from_x)
    both(2, o_from_y)
    both(2, o_from_d)
    if line > 3:
        both(3, o_from_z)

    @pl.when(same)
    def _():
        for h in (2 * (1 - y) + x, 2 * y + 1 - x, 2 * (1 - y) + 1 - x):
            a_pass(h).wait_recv()
            a_pass(h).start()

    @pl.when(other)
    def _():
        for h in range(heads):
            a_pass(h).wait_recv()

        for h in range(heads):
            r_copy(h).wait_recv()

    def emit(n):
        at = pl.ds(pl.multiple_of(n * cut, 128), cut)
        acc = jnp.zeros((rows, cut), F32)
        for h in range(heads):
            acc += lax.dot_general(
                ATT[h], WO[h, at, :], (((1,), (1,)), ((), ())), preferred_element_type=F32
            )
        PR[n] = acc
        DEN[0:rows, 0:1] += jnp.sum(acc * acc, axis=1, keepdims=True)

    DEN[...] = jnp.zeros_like(DEN)
    for k in range(line):
        if k == 3:
            both(3, o_from_x)
            both(3, o_from_y)
            both(3, o_from_d)
        both(k, o_from_c)
        both(k, emit)
    scale = lax.rsqrt(DEN[0:rows, 0:1] / width + EPS)
    kept = other.astype(jnp.int32)

    for h in range(heads):
        at = slice(h * cut, (h + 1) * cut)
        out[:, at] = (
            X[kept, h].astype(F32) + PR[h] * scale * post[at][None, :]
        ).astype(BF16)

    for stream in (segs, ws, kvs):
        stream.drain()
    t_copy(1).wait_send()
    t_copy(2).wait_send()
    t_copy(3).wait_send()

    @pl.when(other)
    def _():
        swap.wait_send()
        t_copy(0).wait_send()
        a_copy(2).wait_send()
        a_copy(3).wait_send()

    @pl.when(same)
    def _():
        a_copy(0).wait_send()
        a_copy(1).wait_send()
        for h in (2 * (1 - y) + x, 2 * y + 1 - x, 2 * (1 - y) + 1 - x):
            a_pass(h).wait_send()
        for h in range(heads):
            r_copy(h).wait_send()

    for zz in range(line):
        @pl.when((zz <= z) & (z < line - 1))
        def _():
            o_copy("up", zz, (0, 0)).wait_send()

        @pl.when((zz >= z) & (z > 0))
        def _():
            o_copy("down", zz, (0, 0)).wait_send()

        o_copy("x", zz, (0, 0)).wait_send()
        o_copy("y", zz, (0, 0)).wait_send()
        if zz % 2 == 1:
            o_copy("y", zz, (1, 0)).wait_send()
        else:
            o_copy("x", zz, (0, 1)).wait_send()
        for rel in ((0, 0), (1, 0), (0, 1), (1, 1)):
            o_copy("c", zz, rel).wait_send()


def fused(tokens, segments, pre_gain, post_gain, w_query, w_key, w_value, w_out):
    seq, heads = lax.axis_size("seq"), lax.axis_size("head")
    rows, cut = tokens.shape
    width = cut * heads
    deep = width // seq
    line = seq // 2
    qd, kd = w_query.shape[1], w_key.shape[1]
    most = rows * seq // 2
    half = HD // 2
    freq = np.float32(10000.0) ** (-(np.arange(half, dtype=np.float32) / np.float32(half)))
    freq = np.concatenate([freq, freq])[None, :].astype(np.float32)
    hbm = pl.BlockSpec(memory_space=pl.ANY)
    vmem = pl.BlockSpec(memory_space=pltpu.VMEM)
    dma = pltpu.SemaphoreType.DMA
    return pl.pallas_call(
        functools.partial(kernel, seq, heads, rows, width, most),
        out_shape=jax.ShapeDtypeStruct((rows, width), BF16),
        in_specs=[hbm] * 9,
        out_specs=vmem,
        scratch_shapes=[
            pltpu.VMEM((rows, cut), BF16),
            pltpu.VMEM((2, heads, rows, cut), BF16),
            pltpu.VMEM((heads, rows, cut), BF16),
            pltpu.VMEM((deep, qd + 2 * kd), BF16),
            pltpu.VMEM((width, qd + 2 * kd), BF16),
            pltpu.VMEM((heads, width, w_out.shape[0]), BF16),
            pltpu.VMEM((seq, 1, rows), jnp.int32),
            pltpu.VMEM((seq, rows, 2 * HD), BF16),
            pltpu.VMEM((rows, GROUP * HD), BF16),
            pltpu.VMEM((heads, rows, GROUP * HD), BF16),
            pltpu.VMEM((heads, rows, cut), F32),
            pltpu.VMEM((rows, qd + 2 * kd), F32),
            pltpu.VMEM((GROUP * rows, HD), BF16),
            pltpu.VMEM((GROUP * rows, HD), F32),
            pltpu.VMEM((GROUP * rows, HD), F32),
            pltpu.VMEM((width,), F32),
            pltpu.VMEM((width,), F32),
            pltpu.VMEM((1, HD), F32),
            dma((10,)),
            dma((heads,)), dma((4,)), dma((heads,)), dma((heads,)),
            dma((seq,)), dma((3, line)),
            dma((seq,)), dma((3, line)), dma((1,)),
            dma((seq, heads)), dma((2, line)), dma((2, line)), dma((2, line)), dma((4, line)),
            dma((seq,)), dma((3, line)),
            dma((heads,)), dma((4,)), dma((heads,)),
        ],
        compiler_params=pltpu.CompilerParams(
            collective_id=0, has_side_effects=True, vmem_limit_bytes=56 * 2**20
        ),
    )(
        tokens, segments[None, :], w_query, w_key, w_value, w_out.T,
        pre_gain, post_gain, freq,
    )


def solution(mesh):
    specs = (
        P("seq", "head"),
        P("seq"),
        P(),
        P(),
        P("seq", "head"),
        P("seq", "head"),
        P("seq", "head"),
        P("head", "seq"),
    )

    def run(*args):
        small = fits(mesh, args[0].shape, args[5].shape, args[7].shape)
        return jax.shard_map(
            fused if small else local,
            mesh=mesh,
            in_specs=specs,
            out_specs=P("seq", None),
            check_vma=False,
        )(*args)

    return run
```

time: 123 us -> 124 us (level)
  Pallas kernels: 117 us -> 121 us
  local copies, waits for them, and re-layouts: 5.9 us -> 3.22 us
    pallas_call x1, Pallas kernels: 117 us -> 121 us  [fused(): pl.pallas_call(functools.partial(kernel, seq, heads, rows, width, most),...]
    broadcast_in_dim x2 -> x0, local copies, waits for them, and re-layouts: 2.68 us -> none  [the longest x1 1.35 us: fused(): pre_gain[None, :]]
where the time goes in v1:
time: 124 us
  Pallas kernels  121 us (98%)
  local copies, waits for them, and re-layouts  3.22 us (3%)
    pallas_call x1, Pallas kernels, fused(): pl.pallas_call(functools.partial(kernel, seq, heads, rows, width, most),...  121 us
    unnamed x1, local copies, waits for them, and re-layouts  3.22 us

profile of v1, /device:TPU:29, one launch (start us, length us, event | category | flops | bytes accessed | tf_op | source)
XLA Modules:
  0.0 124.1 jit_solution(2277836902279507555)
XLA Ops:
  0.0 120.9 %shard_map.91 = bf16[256,4608]{1,0:T(8,128)(2,1)} custom-call(bf16[256,1152]{1,0:T(8,128)(2,1)} %tok.1, s32[1,256]{1,0:T(1,128)} %bitcast.3, bf16[576,256]{1,0:T(8,128)(2,1)} %wq.1, bf16[576,128]{1,0:T(8,128)(2,1)} %wk.1, bf16[576,128]{1,0:T(8,128)(2,1)} %wv.1, bf16[576,256]{1,0:T(8,128)(2,1)} %bitcast.2, f32[4608]{0:T(1024)} %pre_in.1, f32[4608]{0:T(1024)} %post_in.1, ...), custom_call_target="tpu_custom_call" | custom-call | tf_op jit(solution)/shard_map/pallas_call | solution.py:723
  120.9 3.2 %copy.11 = bf16[256,4608]{1,0:T(8,128)(2,1)} copy(bf16[256,4608]{1,0:T(8,128)(2,1)} %shard_map.91) | data formatting | bytes 4718592

commit v2 on v0

v2 whole, which is shorter than its diff:
```python
import enum
import functools

import jax
import jax.numpy as jnp
import numpy as np
from jax import lax
from jax.experimental import pallas as pl
from jax.experimental.pallas import tpu as pltpu
from jax.sharding import PartitionSpec as P

HD = 128
GROUP = 2
SCALAR = 144
DOCS = 8


EPS = 1e-06
CAP = 50.0


def carried_in(value, axis, join, neutral):
    count, mine = (lax.axis_size(axis), lax.axis_index(axis))
    pieces = lax.all_gather(value, axis)
    subtotal = jnp.full_like(value, 0) + jnp.asarray(neutral, value.dtype)

    def step(position, subtotal):
        longer = join(subtotal, pieces[position])
        return jnp.where(position < mine, longer, subtotal)

    return lax.fori_loop(0, count - 1, step, subtotal)


def rotate(values, position, width):
    count = values.shape[1] // width
    half = width // 2
    shaped = values.reshape(values.shape[0], count, width)
    freq = 10000.0 ** (-(jnp.arange(half, dtype=jnp.float32) / half))
    angle = position[:, None] * freq[None, :]
    cosine = jnp.cos(angle)[:, None, :]
    sine = jnp.sin(angle)[:, None, :]
    first = shaped[:, :, :half]
    second = shaped[:, :, half:]
    turned = jnp.concatenate(
        [first * cosine - second * sine, second * cosine + first * sine], axis=2
    )
    return turned.reshape(values.shape[0], count * width)


def add_counts(earlier, later):
    return earlier + later


def local(tokens, segments, pre_gain, post_gain, w_query, w_key, w_value, w_out):
    rows = tokens.shape[0]
    whole = lax.all_gather(tokens, "head", axis=1, tiled=True)
    wide = whole.astype(jnp.float32)
    normed = (
        wide * lax.rsqrt(jnp.mean(wide * wide, axis=1, keepdims=True) + EPS) * pre_gain
    ).astype(jnp.bfloat16)
    pieces = (
        lax.all_gather(w_query, "seq", axis=0, tiled=True),
        lax.all_gather(w_key, "seq", axis=0, tiled=True),
        lax.all_gather(w_value, "seq", axis=0, tiled=True),
    )
    query, key_proj, value_proj = tuple(
        (jnp.dot(normed, piece, preferred_element_type=jnp.float32) for piece in pieces)
    )
    levels = jnp.arange(DOCS, dtype=jnp.int32)
    below = jnp.sum((levels[None, :] > segments[:, None]).astype(jnp.float32), axis=0)
    earlier = carried_in(below, "seq", add_counts, jnp.zeros((DOCS,), jnp.float32))
    starts = earlier + below
    onehot = (segments[:, None] == levels[None, :]).astype(jnp.float32)
    tok_start = jnp.sum(onehot * starts[None, :], axis=1)
    offset = lax.axis_index("seq") * rows
    index_f = (offset + jnp.arange(rows, dtype=jnp.int32)).astype(jnp.float32)
    position = index_f - tok_start
    kv_count = w_key.shape[1] // HD
    rq = (rotate(query, position, HD) * SCALAR ** (-0.5)).astype(jnp.bfloat16)
    rk = rotate(key_proj, position, HD).astype(jnp.bfloat16)
    vb = value_proj.astype(jnp.bfloat16)
    stacked = (
        rq.reshape(rows, kv_count, GROUP, HD)
        .transpose(1, 2, 0, 3)
        .reshape(kv_count, GROUP * rows, HD)
    )
    query_start = jnp.tile(tok_start, GROUP)
    query_index = jnp.tile(index_f, GROUP)
    empty = (
        jnp.zeros((kv_count, GROUP * rows, HD), jnp.float32),
        jnp.zeros((kv_count, GROUP * rows), jnp.float32),
    )
    keys_all = lax.all_gather(rk, "seq", axis=0, tiled=True)
    values_all = lax.all_gather(vb, "seq", axis=0, tiled=True)
    count = keys_all.shape[0]
    block = 1024
    steps_total = count // block

    def compute(offset_blk, state):
        numer, denom = state
        keys_blk = lax.dynamic_slice_in_dim(keys_all, offset_blk, block, 0).reshape(
            block, kv_count, HD
        )
        values_blk = lax.dynamic_slice_in_dim(values_all, offset_blk, block, 0).reshape(
            block, kv_count, HD
        )
        key_index = (offset_blk + jnp.arange(block, dtype=jnp.int32)).astype(jnp.float32)
        scores = jnp.einsum("cqd,kcd->cqk", stacked, keys_blk, preferred_element_type=jnp.float32)
        capped = CAP * jnp.tanh(scores / CAP)
        allowed = (key_index[None, None, :] >= query_start[None, :, None]) & (
            key_index[None, None, :] <= query_index[None, :, None]
        )
        weights = jnp.where(allowed, jnp.exp(capped), 0.0)
        numer = numer + jnp.einsum(
            "cqk,kcd->cqd",
            weights.astype(jnp.bfloat16),
            values_blk,
            preferred_element_type=jnp.float32,
        )
        denom = denom + jnp.sum(weights, axis=2)
        return (numer, denom)

    def one_block(step, state):
        offset_blk = step * block
        return compute(offset_blk, state)

    numer, denom = lax.fori_loop(0, steps_total, one_block, empty)
    attn = (numer / denom[:, :, None]).reshape(kv_count, GROUP, rows, HD).transpose(2, 0, 1, 3)
    attn = attn.reshape(rows, kv_count * GROUP * HD).astype(jnp.bfloat16)
    partial_proj = jnp.dot(
        attn, lax.all_gather(w_out, "seq", axis=1, tiled=True), preferred_element_type=jnp.float32
    )
    partial_proj = lax.optimization_barrier(partial_proj.astype(jnp.bfloat16)).astype(jnp.float32)
    summed = lax.psum(partial_proj.astype(jnp.bfloat16), "head").astype(jnp.float32)
    scale = lax.rsqrt(jnp.mean(summed * summed, axis=1, keepdims=True) + EPS)
    return (wide + summed * scale * post_gain).astype(jnp.bfloat16)


MESH = pl.DeviceIdType.MESH
BF16 = jnp.bfloat16
F32 = jnp.float32
LINE = 4
REACH = LINE // 2
PIECES = 1
OVER_X = (0,)

class E(enum.Enum):
    K1 = enum.auto()
    K2 = enum.auto()
    Kp = enum.auto()
    Od0 = enum.auto()
    Od1 = enum.auto()
    Od2 = enum.auto()
    Od3 = enum.auto()
    On0 = enum.auto()
    On1 = enum.auto()
    On2 = enum.auto()
    On3 = enum.auto()
    Ox0 = enum.auto()
    Ox1 = enum.auto()
    Ox2 = enum.auto()
    Ox3 = enum.auto()
    Oy0 = enum.auto()
    Oy1 = enum.auto()
    Oy2 = enum.auto()
    Oy3 = enum.auto()
    Pk = enum.auto()
    Pq = enum.auto()
    Sh0 = enum.auto()
    Sh1 = enum.auto()
    Sh2 = enum.auto()
    Sh3 = enum.auto()
    Sk = enum.auto()
    Sq = enum.auto()
    TF = enum.auto()
    Tp = enum.auto()
    Tx = enum.auto()
    Ty = enum.auto()
    W0k = enum.auto()
    W0q = enum.auto()
    Wk1 = enum.auto()
    Wk2 = enum.auto()
    Wk3 = enum.auto()
    Wq1 = enum.auto()
    Wq2 = enum.auto()
    Wq3 = enum.auto()


PLAN = {
    (0, 0): (
        (E.Tp, E.W0q, E.Ty, E.On0, E.W0k,),
        (E.Sh0, E.Tx, E.On1, E.TF, E.Sh1, E.Wk1, E.Wq2, E.Oy1, E.Wk3, E.Sq, E.On2, E.Sh2, E.Sk, E.Oy0, E.Wq1, E.Wk2, E.Ox1, E.Wq3,),
        (E.Pk,),
        (E.K1, E.Ox2, E.On3, E.Ox0, E.Oy2, E.Sh3, E.Oy3, E.Pq, E.Od0, E.Od2, E.Od1,),
        (E.K2, E.Kp,),
        (),
        (E.Ox3,),
        (),
        (),
        (E.Od3,),
    ),
    (0, 1): (
        (E.Ty, E.W0k, E.On0, E.Tx, E.Sh0, E.Ox0,),
        (E.Tp, E.W0q, E.TF, E.On1, E.Sh1, E.Sk, E.On2, E.Wk2, E.Wk1, E.Sh2,),
        (E.Wk3, E.Sq, E.Wq1, E.K1, E.Pk, E.Ox1, E.Oy1, E.Oy0, E.Od0,),
        (E.K2, E.Wq2, E.Wq3, E.Ox2, E.Kp, E.Pq,),
        (E.Ox3, E.On3, E.Sh3, E.Od1,),
        (E.Od2, E.Od3, E.Oy2,),
        (),
        (E.Oy3,),
        (),
        (),
    ),
    (1, 0): (
        (E.Oy3, E.Ty, E.Tp, E.W0k, E.W0q,),
        (E.On0, E.TF, E.Wk1, E.Tx, E.Sq, E.Wq1, E.On1, E.Sh0, E.Ox0, E.Sh1, E.Sk, E.Wk3, E.Od0, E.Oy0, E.Wk2, E.Oy1, E.On3, E.Pk, E.Wq3, E.Wq2, E.On2, E.Pq, E.Ox1,),
        (E.Sh2, E.K1,),
        (E.Od1,),
        (E.Od3, E.K2, E.Kp,),
        (),
        (E.Oy2, E.Ox2,),
        (E.Od2, E.Sh3,),
        (E.Ox3,),
        (),
    ),
    (1, 1): (
        (E.W0k, E.Ty, E.On0, E.Tp, E.Tx, E.Oy3, E.W0q, E.Od3, E.Sh0,),
        (E.Sk, E.Wk1, E.On1, E.On3, E.TF, E.Wk3, E.Wk2, E.Sq,),
        (E.Sh1, E.Wq1, E.Ox1, E.Pk, E.Wq2,),
        (E.Oy1, E.Ox0, E.On2, E.Ox3, E.K2, E.Wq3, E.Pq, E.Sh2,),
        (E.K1, E.Kp, E.Od1,),
        (),
        (E.Oy0, E.Ox2, E.Sh3, E.Oy2, E.Od0,),
        (),
        (E.Od2,),
        (),
    ),
    (2, 0): (
        (E.Oy3, E.Ty, E.Tp, E.W0k, E.On0, E.W0q, E.Ox3, E.Wk1, E.On3, E.TF, E.Tx, E.Sh0,),
        (E.Sk, E.On1, E.Wk3, E.Wk2, E.Sh1, E.Wq2, E.Wq1, E.Oy0,),
        (E.Oy1, E.On2, E.Ox1, E.Pk, E.Ox0, E.Sq,),
        (E.Sh2, E.Wq3, E.Pq, E.K2, E.Od0,),
        (E.K1, E.Kp, E.Od1, E.Od3, E.Oy2, E.Ox2,),
        (E.Sh3,),
        (),
        (),
        (E.Od2,),
        (),
    ),
    (2, 1): (
        (E.Oy3, E.Ty, E.W0k, E.Tx, E.Tp, E.On0, E.Sh0, E.W0q, E.Sk, E.TF, E.Wk1, E.On1, E.Sh1,),
        (E.Wk2, E.Ox0, E.On3, E.Wk3,),
        (E.Sq, E.Wq1, E.Wq3, E.Pk, E.Wq2, E.Oy1, E.Pq,),
        (E.Ox1, E.Od0, E.On2, E.K1,),
        (E.Sh2, E.Oy0, E.K2, E.Kp, E.Od3,),
        (E.Ox2, E.Od1, E.Od2, E.Ox3, E.Oy2,),
        (),
        (),
        (),
        (E.Sh3,),
    ),
    (3, 0): (
        (E.W0k, E.Tp, E.Wk1, E.On0,),
        (E.Ty, E.Sh0, E.W0q, E.Tx, E.On1, E.TF, E.Sh1, E.On2,),
        (E.Wq1, E.Wk3, E.Sh2, E.Wk2, E.Sq, E.Oy1, E.Oy0, E.Ox0, E.Ox1, E.Wq3, E.On3, E.Sk, E.Sh3, E.Ox2, E.Pk, E.K1,),
        (E.Od0, E.Oy3, E.Wq2, E.Oy2, E.Pq, E.K2, E.Kp,),
        (E.Od2,),
        (E.Od1,),
        (),
        (E.Ox3,),
        (),
        (E.Od3,),
    ),
    (3, 1): (
        (),
        (E.W0k, E.Ty, E.On0, E.Tp, E.Tx, E.W0q, E.Sh0, E.TF, E.On1, E.Wk2, E.Sk, E.On2, E.Sh1, E.Sq, E.Ox0, E.Wk1, E.Sh2, E.Oy2, E.Wk3, E.Pk, E.Ox1, E.Oy0, E.Wq2, E.Od0,),
        (E.Oy1, E.Ox2, E.Wq1, E.Wq3,),
        (E.On3, E.Pq, E.Sh3, E.K1,),
        (E.K2, E.Kp, E.Od1, E.Od2,),
        (E.Oy3, E.Ox3, E.Od3,),
        (),
        (),
        (),
        (),
    ),
}


def fits(mesh, tokens, w_key, w_out):
    seq, head = mesh.shape["seq"], mesh.shape["head"]
    width = tokens[1]
    weights = 2 * width * (w_key[1] // head) * (GROUP + 2)
    outs = 2 * w_out[0] * width
    rows = tokens[0] // seq
    rest = rows * width * (4 + 2 + 4 + 2) + tokens[0] * (w_key[1] // head) * 4
    return (
        head == 4
        and seq == 2 * LINE
        and w_key[1] // head == HD
        and (width // head) % 128 == 0
        and (width // seq) % (16 * PIECES) == 0
        and weights + outs + rest < 44 * 2**20
    )


def sides(z, k, down=True):
    return [z] if k == 0 else [at for at in (z - k, z + k if down else -1) if 0 <= at < LINE]


class Moves:
    def __init__(self, z, kind, e):
        self.z, self.kind, self.e = z, kind, e
        x, y = e.x, e.y
        c = x if kind == 0 else 1 - x
        self.x, self.y, self.c = x, y, c
        self.me, self.head = 2 * z + x, 2 * y + c
        self.partner = (self.me, 2 * y + 1 - c)
        self.xn = (2 * z + 1 - x, self.head)
        self.yn = (self.me, 2 * (1 - y) + c)
        self.hg = 2 * y + x

    def remote(self, src, dst, send, recv, where):
        return pltpu.make_async_remote_copy(
            src_ref=src, dst_ref=dst, send_sem=send, recv_sem=recv,
            device_id=where, device_id_type=MESH,
        )

    def w_ref(self, b, part):
        e = self.e
        rows = pl.ds(pl.multiple_of(b * e.deep, 16), e.deep)
        return e.W.at[rows, pl.ds(part * e.qd, e.qd)]

    def w_copy(self, part, zz, way):
        e = self.e
        b = 2 * zz + self.c
        where = ((self.me + 2, self.head), (self.me - 2, self.head), self.partner)[way]
        ref = self.w_ref(b, part)
        return self.remote(ref, ref, e.w_send, e.w_recv.at[part, LINE if way == 2 else zz], where)

    def w_onward(self, part, zz):
        return [
            self.w_copy(part, zz, way)
            for way, told in (
                (0, zz <= self.z < LINE - 1), (1, zz >= self.z > 0), (2, True),
            )
            if told
        ]

    def w_swap(self, part):
        e = self.e
        return self.remote(
            e.SW.at[:, pl.ds(part * e.qd, e.qd)], self.w_ref(self.me, part),
            e.w_send, e.w_recv.at[part, self.z], (2 * self.z + self.c, self.hg),
        )

    def w_take(self, part, zz):
        self.remote_take(self.w_ref(2 * zz + self.c, part), self.e.w_recv.at[part, zz])

    def w_beside(self, part):
        self.remote_take(self.units(LINE), self.e.w_recv.at[part, LINE])

    def units(self, n):
        return self.e.WO.at[pl.ds(0, n * self.e.deep)]

    def remote_take(self, ref, recv):
        self.remote(ref, ref, self.e.w_send, recv, self.partner).wait_recv()

    def remote_left(self, ref, send):
        self.remote(ref, ref, send, self.e.w_recv.at[0, 0], self.partner).wait_send()

    def k_copy(self, zz, way):
        e = self.e
        b = 2 * zz + self.c
        where = ((self.me + 2, self.head), self.partner)[way]
        return self.remote(e.KV.at[b], e.KV.at[b], e.k_send, e.k_recv.at[LINE if way else zz], where)

    def k_onward(self, zz):
        up = zz <= self.z < LINE - 1 and self.z - zz < REACH
        return ([self.k_copy(zz, 0)] if up else []) + [self.k_copy(zz, 1)]

    def k_take(self, zz):
        self.remote_take(self.e.KV.at[2 * zz + self.c], self.e.k_recv.at[zz])

    def k_beside(self):
        n = self.z + 1 - max(self.z - REACH, 0)
        self.remote_take(self.e.KV.at[pl.ds(0, n)], self.e.k_recv.at[LINE])

    def t_copy(self, way):
        e = self.e
        where = (
            self.partner,
            (2 * self.z + 1 - self.x, 2 * self.y + self.x),
            (self.me, 2 * (1 - self.y) + self.x),
        )[way]
        return self.remote(e.TOK, e.X.at[0, self.head], e.t_send, e.t_recv.at[self.head], where)

    def t_take(self, h):
        self.remote_take(self.e.X.at[0, h], self.e.t_recv.at[h])

    def t_relay(self):
        e = self.e
        h, where = ((2 * (1 - self.y) + self.x, self.xn), (2 * self.y + self.x, self.yn))[self.kind]
        return h, self.remote(e.X.at[0, h], e.X.at[0, h], e.t_send, e.t_recv.at[h], where)

    def r_copy(self, h):
        e = self.e
        return self.remote(e.X.at[0, h], e.X.at[1, h], e.r_send, e.r_recv, self.partner)

    def o_copy(self, way, zz, fx, fy, i):
        e = self.e
        b = 2 * zz + (1 - self.x if fx else self.x)
        h = 2 * (1 - self.y) + self.c if fy else self.head
        if way == "c":
            send, recv, where = e.oc_send, e.o_side.at[zz], self.partner
        else:
            fx, fy, where = {
                "up": (fx, fy, (self.me + 2, self.head)),
                "down": (fx, fy, (self.me - 2, self.head)),
                "x": (1, fy, self.xn),
                "y": (fx, 1, self.yn),
            }[way]
            send, recv = e.o_send, e.o_recv.at[2 * fx + fy, zz, i]
        ref = self.o_ref(b, h, i)
        return self.remote(ref, ref, send, recv, where)

    def o_ref(self, b, h, i):
        e = self.e
        piece = e.deep // PIECES
        at = (h * 2 * LINE + b) * e.deep + i * piece
        return e.WO.at[pl.ds(pl.multiple_of(at, 16), piece)]

    def o_onward(self, zz, i):
        return [
            self.o_copy(way, zz, 0, 0, i)
            for way, told in (("up", zz <= self.z < LINE - 1), ("down", zz >= self.z > 0))
            if told
        ]

    def o_share(self, zz, i):
        return [self.o_copy(way, zz, 0, 0, i) for way in ("x", "y", "c")]

    def o_from_x(self, zz, i):
        turn = [self.o_copy("y", zz, 1, 0, i)] if zz not in OVER_X else []
        return turn + [self.o_copy("c", zz, 1, 0, i)]

    def o_from_y(self, zz, i):
        turn = [self.o_copy("x", zz, 0, 1, i)] if zz in OVER_X else []
        return turn + [self.o_copy("c", zz, 0, 1, i)]

    def o_take(self, zz, fx, fy, i):
        self.remote_take(self.o_ref(0, 0, i), self.e.o_recv.at[2 * fx + fy, zz, i])

    def o_beside(self, zz):
        self.remote_take(self.units(4), self.e.o_side.at[zz])

    def a_copy(self, way):
        e = self.e
        where = (
            self.partner, self.yn, self.xn, (2 * self.z + 1 - self.x, 2 * (1 - self.y) + self.c),
        )[way]
        return self.remote(e.AO, e.ATT.at[self.hg], e.a_send, e.a_recv.at[0 if way == 0 else self.hg], where)

    def a_ways(self):
        return (1, 0) if self.kind == 0 else (2, 3)

    def a_pass(self, h):
        e = self.e
        return self.remote(e.ATT.at[h], e.ATT.at[h], e.a_send, e.a_recv.at[0], self.partner)

    def a_far(self):
        x, y = self.x, self.y
        return (2 * (1 - y) + x, 2 * y + 1 - x, 2 * (1 - y) + 1 - x)

    def do(self, event):
        z, kind, e = self.z, self.kind, self.e
        event = event.name
        name, k = event[:-1], event[-1]
        begin = lambda copies: [copy.start() for copy in copies]
        if name == "W0":
            part = "qk".index(k)
            for move in e.w_loads[kind][part]:
                move.wait()
            begin(self.w_onward(part, z) if kind == 0 else [self.w_swap(part)])
        elif name == "S":
            if kind == 1:
                part = "qk".index(k)
                self.w_take(part, z)
                begin(self.w_onward(part, z))
        elif name in ("Wq", "Wk"):
            part = "qk".index(name[1])
            for zz in sides(z, int(k)):
                self.w_take(part, zz)
                begin(self.w_onward(part, zz))
        elif name == "P":
            self.w_beside("qk".index(k))
        elif event in ("Tp", "Tx", "Ty"):
            if (z, kind) not in e.loaded:
                e.loaded.add((z, kind))
                e.l_tok.wait()
            if event != "Tp" or kind == 1:
                self.t_copy("pxy".index(event[1])).start()
        elif event == "TF":
            h, relay = self.t_relay()
            self.t_take(h)
            relay.start()
        elif name == "On":
            for zz in sides(z, int(k)):
                for i in range(PIECES):
                    if zz != z:
                        self.o_take(zz, 0, 0, i)
                    elif i == 0:
                        e.l_out.wait()
                    begin(self.o_onward(zz, i))
        elif name == "Sh":
            for zz in sides(z, int(k)):
                for i in range(PIECES):
                    begin(self.o_share(zz, i))
        elif name in ("Ox", "Oy", "Od"):
            fx, fy = {"x": (1, 0), "y": (0, 1), "d": (1, 1)}[name[1]]
            for zz in sides(z, int(k)):
                for i in range(PIECES):
                    self.o_take(zz, fx, fy, i)
                    if fx and fy:
                        self.o_copy("c", zz, 1, 1, i).start()
                    else:
                        begin(self.o_from_x(zz, i) if fx else self.o_from_y(zz, i))
        elif event == "Kp":
            self.k_beside()
        elif name == "K":
            for zz in sides(z, int(k), False):
                self.k_take(zz)
                begin(self.k_onward(zz))
        else:
            raise ValueError(event)

    def tokens(self):
        e = self.e
        x, y = self.x, self.y
        if self.kind == 0:
            e.l_own.wait()
            self.t_take(2 * y + 1 - x)
            self.t_take(2 * (1 - y) + 1 - x)
            for h in range(4):
                self.r_copy(h).start()
        else:
            self.t_take(2 * y + 1 - x)
            self.t_take(2 * (1 - y))
            self.t_take(2 * (1 - y) + 1)

    def attended(self):
        for way in self.a_ways():
            self.a_copy(way).start()

    def gathered(self):
        e = self.e
        if self.kind == 0:
            for h in self.a_far():
                self.remote_take(e.ATT.at[h], e.a_recv.at[h])
                self.a_pass(h).start()
        else:
            self.remote_take(e.ATT, e.a_recv.at[0])
            self.remote_take(e.X.at[1], e.r_recv)

    def emitted(self, k):
        for zz in sides(self.z, k):
            self.o_beside(zz)

    def drain(self):
        z, kind, e = self.z, self.kind, self.e
        weights = sum(len(self.w_onward(part, zz)) for part in range(2) for zz in range(LINE))
        self.remote_left(self.units(weights + 2 * kind), e.w_send)
        outs = sum(
            len(self.o_onward(zz, 0)) + 2 + len(self.o_from_x(zz, 0)) + len(self.o_from_y(zz, 0)) - 2
            for zz in range(LINE)
        )
        self.remote_left(self.units(outs), e.o_send)
        self.remote_left(self.units(4 * LINE), e.oc_send)
        keys = sum(len(self.k_onward(zz)) for zz in range(max(z - REACH, 0), z + 1))
        self.remote_left(e.KV.at[pl.ds(0, keys)], e.k_send)
        self.remote_left(e.X.at[0, pl.ds(0, 3 + kind)], e.t_send)
        self.remote_left(e.KV.at[pl.ds(0, 2 if kind else 5)], e.a_send)
        if kind == 0:
            self.remote_left(e.X.at[0], e.r_send)


class Names:
    pass


def kernel(
    seq, heads, rows, width, most,
    tok, seg_row, wq, wk, wv, wo_in, pre_in, post_in, freq_in,
    out,
    TOK, X, XN, SW, W, WO, SEG, KV, AO, ATT, PR, RQ, NUM, DEN, pre1, post1, pre, post, freq,
    loc, t_recv, t_send, r_recv, r_send, s_recv, s_send, w_recv, w_send,
    o_recv, o_side, o_send, oc_send, k_recv, k_send, a_recv, a_send,
):
    me, head = lax.axis_index("seq"), lax.axis_index("head")
    z, x = me // 2, lax.rem(me, 2)
    y, c = head // 2, lax.rem(head, 2)
    deep = width // seq
    cut = width // heads
    qd, kd = wq.shape[1], wk.shape[1]
    same = c == x
    other = c != x
    rb = 2 * z + c
    hg = 2 * y + x

    e = Names()
    e.x, e.y, e.deep, e.qd = x, y, deep, qd
    e.loaded = set()
    e.TOK, e.X, e.SW, e.W, e.WO, e.KV, e.AO, e.ATT = TOK, X, SW, W, WO, KV, AO, ATT
    e.t_recv, e.t_send, e.r_recv, e.r_send = t_recv, t_send, r_recv, r_send
    e.w_recv, e.w_send, e.o_recv, e.o_side = w_recv, w_send, o_recv, o_side
    e.o_send, e.oc_send = o_send, oc_send
    e.k_recv, e.k_send, e.a_recv, e.a_send = k_recv, k_send, a_recv, a_send

    def load_weights(block):
        return (
            [pltpu.make_async_copy(wq, block.at[:, pl.ds(0, qd)], loc.at[4])],
            [
                pltpu.make_async_copy(wk, block.at[:, pl.ds(qd, kd)], loc.at[5]),
                pltpu.make_async_copy(wv, block.at[:, pl.ds(qd + kd, kd)], loc.at[6]),
            ],
        )

    mine = pl.ds(pl.multiple_of(me * deep, 16), deep)
    e.w_loads = (load_weights(W.at[mine]), load_weights(SW))
    e.l_tok = pltpu.make_async_copy(tok, TOK, loc.at[0])
    e.l_own = pltpu.make_async_copy(tok, X.at[0, head], loc.at[1])
    l_seg = pltpu.make_async_copy(seg_row, SEG.at[me], loc.at[2])
    place = pl.ds(pl.multiple_of((head * seq + me) * deep, 16), deep)
    e.l_out = pltpu.make_async_copy(wo_in, WO.at[place], loc.at[3])
    small = [
        pltpu.make_async_copy(pre_in, pre1, loc.at[7]),
        pltpu.make_async_copy(post_in, post1, loc.at[8]),
        pltpu.make_async_copy(freq_in, freq, loc.at[9]),
    ]

    for kind, told in enumerate((same, other)):
        @pl.when(told)
        def _():
            for part in (1, 0):
                for move in e.w_loads[kind][part]:
                    move.start()

    l_seg.start()
    e.l_tok.start()
    e.l_out.start()

    @pl.when(same)
    def _():
        e.l_own.start()

    for move in small:
        move.start()

    barrier = pltpu.get_barrier_semaphore()

    def greet(where):
        pl.semaphore_signal(barrier, inc=1, device_id=where, device_id_type=MESH)

    for dx in range(2):
        for dy in range(2):
            for dc in range(2):
                if dy + dc > 0:
                    gx = lax.rem(x + dx, 2)
                    greet((2 * z + gx, 2 * lax.rem(y + dy, 2) + lax.rem(c + dc, 2)))
    for d in range(1, seq):
        greet((lax.rem(me + d, seq), head))
    pl.semaphore_wait(barrier, 6 + seq - 1)

    l_seg.wait()

    def s_copy(d):
        return pltpu.make_async_remote_copy(
            src_ref=SEG.at[me], dst_ref=SEG.at[me], send_sem=s_send, recv_sem=s_recv,
            device_id=(lax.rem(me + d, seq), head), device_id_type=MESH,
        )

    def s_all():
        ref = SEG.at[pl.ds(0, seq - 1)]
        return pltpu.make_async_remote_copy(
            src_ref=ref, dst_ref=ref, send_sem=s_send, recv_sem=s_recv,
            device_id=(lax.rem(me + 1, seq), head), device_id_type=MESH,
        )

    for d in range(1, seq):
        s_copy(d).start()

    def everyone(act):
        for place in range(LINE):
            for kind, told in enumerate((same, other)):
                @pl.when((z == place) & told)
                def _():
                    act(Moves(place, kind, e))

    def events(phase):
        def act(moves):
            for event in PLAN[moves.z, moves.kind][phase]:
                moves.do(event)

        everyone(act)

    events(0)
    s_all().wait_recv()
    for move in small:
        move.wait()
    for h in range(heads):
        at = slice(h * cut, (h + 1) * cut)
        pre[0:1, at] = pre1[at][None, :]
        post[0:1, at] = post1[at][None, :]
    own = jnp.broadcast_to(SEG[rb].astype(F32), (HD, rows))
    col = jnp.transpose(own)[:, 0:1]
    start = jnp.zeros((rows, 1), F32)
    for j in range(seq):
        start += jnp.sum((SEG[j].astype(F32) < col).astype(F32), axis=1, keepdims=True)
    index = (rb * rows + lax.broadcasted_iota(jnp.int32, (rows, 1), 0)).astype(F32)
    angle = (index - start) * freq[...]
    cosine = jnp.cos(angle)
    sine = jnp.sin(angle)
    lane = lax.broadcasted_iota(jnp.int32, (rows, HD), 1)
    sine = jnp.where(lane < HD // 2, -sine, sine)

    events(1)
    everyone(lambda moves: moves.tokens())
    half = rows // 2

    def norm_rows(r, _):
        at = pl.ds(pl.multiple_of(r * half, half), half)
        total = jnp.zeros((half, 1), F32)
        for h in range(heads):
            wide = X[0, h, at, :].astype(F32)
            total += jnp.sum(wide * wide, axis=1, keepdims=True)
        scale = lax.rsqrt(total / width + EPS)
        for h in range(heads):
            gain = pre[0:1, h * cut : (h + 1) * cut]
            XN[h, at, :] = (X[0, h, at, :].astype(F32) * scale * gain).astype(BF16)
        return 0

    lax.fori_loop(0, 2, norm_rows, 0)

    def project(part):
        cols = slice(part * qd, (part + 1) * qd)
        total = jnp.zeros((rows, qd), F32)
        for h in range(heads):
            some = slice(h * cut, (h + 1) * cut)
            total += jnp.dot(XN[h], W[some, cols], preferred_element_type=F32)
        return total

    def turn(values):
        return values * cosine + pltpu.roll(values, HD // 2, 1) * sine

    events(2)
    keyed = project(1)
    KV[rb, :, 0:HD] = turn(keyed[:, 0:HD]).astype(BF16)
    KV[rb, :, HD : 2 * HD] = keyed[:, kd : kd + HD].astype(BF16)
    everyone(lambda moves: [copy.start() for copy in moves.k_onward(moves.z)])
    events(3)
    asked = project(0)
    for g in range(GROUP):
        RQ[g * rows : (g + 1) * rows, :] = (
            turn(asked[:, g * HD : (g + 1) * HD]) * SCALAR ** (-0.5)
        ).astype(BF16)

    events(4)
    start2 = jnp.concatenate([start] * GROUP, axis=0)
    index2 = jnp.concatenate([index] * GROUP, axis=0)
    NUM[...] = jnp.zeros_like(NUM)
    DEN[...] = jnp.zeros_like(DEN)

    def attend(j, _):
        s = lax.dot_general(
            RQ[...], KV[j, :, 0:HD], (((1,), (1,)), ((), ())), preferred_element_type=F32
        )
        at = (j * rows + lax.broadcasted_iota(jnp.int32, (1, rows), 1)).astype(F32)
        p = jnp.where(
            (at >= start2) & (at <= index2), jnp.exp(CAP * jnp.tanh(s * (1.0 / CAP))), 0.0
        )
        DEN[...] += jnp.sum(p, axis=1, keepdims=True)
        NUM[...] += jnp.dot(p.astype(BF16), KV[j, :, HD : 2 * HD], preferred_element_type=F32)
        return 0

    lax.fori_loop(jnp.maximum(rb - most // rows, 0), rb + 1, attend, 0)
    ratio = (NUM[...] / DEN[:, 0:1]).astype(BF16)
    for g in range(GROUP):
        AO[:, g * HD : (g + 1) * HD] = ratio[g * rows : (g + 1) * rows, :]
    everyone(lambda moves: moves.attended())

    @pl.when(same)
    def _():
        for g in range(GROUP):
            ATT[hg, :, g * HD : (g + 1) * HD] = ratio[g * rows : (g + 1) * rows, :]

    events(5)
    everyone(lambda moves: moves.gathered())

    def emit(n):
        acc = jnp.zeros((rows, cut), F32)
        for h in range(heads):
            acc += lax.dot_general(
                ATT[h], WO[pl.ds(pl.multiple_of(h * width + n * cut, 128), cut), :],
                (((1,), (1,)), ((), ())), preferred_element_type=F32,
            )
        PR[n] = acc
        DEN[0:rows, 0:1] += jnp.sum(acc * acc, axis=1, keepdims=True)

    DEN[...] = jnp.zeros_like(DEN)
    for k in range(LINE):
        events(6 + k)
        everyone(lambda moves: moves.emitted(k))
        if k == 0:
            emit(z)
        else:

            @pl.when(z >= k)
            def _():
                emit(z - k)

            @pl.when(z + k < LINE)
            def _():
                emit(z + k)
    scale = lax.rsqrt(DEN[0:rows, 0:1] / width + EPS)
    kept = other.astype(jnp.int32)

    def finish(h, _):
        at = pl.ds(pl.multiple_of(h * cut, 128), cut)
        out[:, at] = (X[kept, h].astype(F32) + PR[h] * scale * post[0:1, at]).astype(BF16)
        return 0

    lax.fori_loop(0, heads, finish, 0)
    everyone(lambda moves: moves.drain())
    s_all().wait_send()


def fused(tokens, segments, pre_gain, post_gain, w_query, w_key, w_value, w_out):
    seq, heads = lax.axis_size("seq"), lax.axis_size("head")
    rows, cut = tokens.shape
    width = cut * heads
    deep = width // seq
    qd, kd = w_query.shape[1], w_key.shape[1]
    most = rows * seq // 2
    half = HD // 2
    freq = np.float32(10000.0) ** (-(np.arange(half, dtype=np.float32) / np.float32(half)))
    freq = np.concatenate([freq, freq])[None, :].astype(np.float32)
    hbm = pl.BlockSpec(memory_space=pl.ANY)
    vmem = pl.BlockSpec(memory_space=pltpu.VMEM)
    dma = pltpu.SemaphoreType.DMA
    return pl.pallas_call(
        functools.partial(kernel, seq, heads, rows, width, most),
        out_shape=pltpu.VMEM((rows, width), BF16),
        in_specs=[hbm] * 9,
        out_specs=vmem,
        scratch_shapes=[
            pltpu.VMEM((rows, cut), BF16),
            pltpu.VMEM((2, heads, rows, cut), BF16),
            pltpu.VMEM((heads, rows, cut), BF16),
            pltpu.VMEM((deep, qd + 2 * kd), BF16),
            pltpu.VMEM((width, qd + 2 * kd), BF16),
            pltpu.VMEM((heads * width, w_out.shape[0]), BF16),
            pltpu.VMEM((seq, 1, rows), jnp.int32),
            pltpu.VMEM((seq, rows, 2 * HD), BF16),
            pltpu.VMEM((rows, GROUP * HD), BF16),
            pltpu.VMEM((heads, rows, GROUP * HD), BF16),
            pltpu.VMEM((heads, rows, cut), F32),
            pltpu.VMEM((GROUP * rows, HD), BF16),
            pltpu.VMEM((GROUP * rows, HD), F32),
            pltpu.VMEM((GROUP * rows, HD), F32),
            pltpu.VMEM((width,), F32),
            pltpu.VMEM((width,), F32),
            pltpu.VMEM((1, width), F32),
            pltpu.VMEM((1, width), F32),
            pltpu.VMEM((1, HD), F32),
            dma((10,)),
            dma((heads,)), dma, dma, dma, dma, dma,
            dma((2, LINE + 1)), dma,
            dma((4, LINE, PIECES)), dma((LINE,)), dma, dma,
            dma((LINE + 1,)), dma, dma((heads,)), dma,
        ],
        compiler_params=pltpu.CompilerParams(
            collective_id=0, has_side_effects=True, vmem_limit_bytes=52 * 2**20
        ),
    )(
        tokens, segments[None, :], w_query, w_key, w_value, w_out.T,
        pre_gain, post_gain, freq,
    )


def solution(mesh):
    specs = (
        P("seq", "head"),
        P("seq"),
        P(),
        P(),
        P("seq", "head"),
        P("seq", "head"),
        P("seq", "head"),
        P("head", "seq"),
    )

    def run(*args):
        small = fits(mesh, args[0].shape, args[5].shape, args[7].shape)
        return jax.shard_map(
            fused if small else local,
            mesh=mesh,
            in_specs=specs,
            out_specs=P("seq", None),
            check_vma=False,
        )(*args)

    return run
```

time: 123 us -> 88.2 us (0.72)
  Pallas kernels: 117 us -> 86.6 us
  local copies, waits for them, and re-layouts: 5.9 us -> 1.41 us
    pallas_call x1, Pallas kernels: 117 us -> 86.6 us  [fused(): pl.pallas_call(functools.partial(kernel, seq, heads, rows, width, most),...]
    broadcast_in_dim x2 -> x0, local copies, waits for them, and re-layouts: 2.68 us -> none  [the longest x1 1.35 us: fused(): pre_gain[None, :]]
    unnamed x1, local copies, waits for them, and re-layouts: 3.22 us -> 1.41 us
where the time goes in v2:
time: 88.2 us; the launch traced here: 88 us
  Pallas kernels  86.6 us (98%)
  local copies, waits for them, and re-layouts  1.41 us (2%)
    pallas_call x1, Pallas kernels, fused(): pl.pallas_call(functools.partial(kernel, seq, heads, rows, width, most),...  86.6 us

profile of v2, /device:TPU:29, one launch (start us, length us, event | category | flops | bytes accessed | tf_op | source)
XLA Modules:
  0.0 88.0 jit_solution(7715273311665399725)
XLA Ops:
  0.0 86.6 %shard_map.91 = bf16[256,4608]{1,0:T(8,128)(2,1)S(1)} custom-call(bf16[256,1152]{1,0:T(8,128)(2,1)} %tok.1, s32[1,256]{1,0:T(1,128)} %bitcast.3, bf16[576,256]{1,0:T(8,128)(2,1)} %wq.1, bf16[576,128]{1,0:T(8,128)(2,1)} %wk.1, bf16[576,128]{1,0:T(8,128)(2,1)} %wv.1, bf16[576,256]{1,0:T(8,128)(2,1)} %bitcast.2, f32[4608]{0:T(1024)} %pre_in.1, f32[4608]{0:T(1024)} %post_in.1, ...), custom_call_target="tpu_custom_call" | custom-call | tf_op jit(solution)/shard_map/pallas_call | solution.py:849
  86.6 1.4 %copy.11 = bf16[256,4608]{1,0:T(8,128)(2,1)} copy(bf16[256,4608]{1,0:T(8,128)(2,1)S(1)} %shard_map.91) | data formatting | bytes 4718592

commit v3 on v2

--- a/solution.py
+++ b/solution.py
@@ -164,8 +164,6 @@
     Oy1 = enum.auto()
     Oy2 = enum.auto()
     Oy3 = enum.auto()
-    Pk = enum.auto()
-    Pq = enum.auto()
     Sh0 = enum.auto()
     Sh1 = enum.auto()
     Sh2 = enum.auto()
@@ -188,96 +186,144 @@
 
 PLAN = {
     (0, 0): (
-        (E.Tp, E.W0q, E.Ty, E.On0, E.W0k,),
-        (E.Sh0, E.Tx, E.On1, E.TF, E.Sh1, E.Wk1, E.Wq2, E.Oy1, E.Wk3, E.Sq, E.On2, E.Sh2, E.Sk, E.Oy0, E.Wq1, E.Wk2, E.Ox1, E.Wq3,),
-        (E.Pk,),
-        (E.K1, E.Ox2, E.On3, E.Ox0, E.Oy2, E.Sh3, E.Oy3, E.Pq, E.Od0, E.Od2, E.Od1,),
-        (E.K2, E.Kp,),
-        (),
+        (E.On0, E.Tp, E.Ty, E.Tx, E.W0q, E.W0k, E.On1, E.Sh1, E.On2, E.TF, E.Sh0, E.Ox1, E.Wk1,),
+        (E.Sk, E.Wq1, E.On3, E.Sh2,),
+        (E.Wk2, E.Sh3, E.Sq, E.Wk3,),
+        (),
+        (),
+        (),
+        (E.Oy0, E.Ox2, E.Wq2, E.Wq3,),
+        (E.K1, E.Od1, E.K2, E.Ox0, E.Od0,),
+        (),
+        (),
+        (E.Oy1, E.Od2, E.Kp,),
+        (E.Oy2, E.Oy3,),
         (E.Ox3,),
         (),
-        (),
         (E.Od3,),
+        (),
     ),
     (0, 1): (
-        (E.Ty, E.W0k, E.On0, E.Tx, E.Sh0, E.Ox0,),
-        (E.Tp, E.W0q, E.TF, E.On1, E.Sh1, E.Sk, E.On2, E.Wk2, E.Wk1, E.Sh2,),
-        (E.Wk3, E.Sq, E.Wq1, E.K1, E.Pk, E.Ox1, E.Oy1, E.Oy0, E.Od0,),
-        (E.K2, E.Wq2, E.Wq3, E.Ox2, E.Kp, E.Pq,),
-        (E.Ox3, E.On3, E.Sh3, E.Od1,),
-        (E.Od2, E.Od3, E.Oy2,),
-        (),
-        (E.Oy3,),
+        (E.On0, E.Tp, E.W0k, E.Ty, E.W0q, E.Sq, E.Sh0, E.On2, E.Sk, E.Wq1, E.Tx, E.On1, E.Ox1, E.Sh1, E.Oy1, E.TF, E.Sh2, E.Wk1, E.Wk3, E.Ox2, E.Oy0,),
+        (E.Wk2, E.Oy2,),
+        (E.Wq2,),
+        (),
+        (E.On3, E.Od1,),
+        (E.Od2, E.Ox0, E.K2, E.K1, E.Wq3,),
+        (),
+        (E.Ox3,),
+        (E.Od0, E.Sh3,),
+        (E.Kp,),
+        (),
+        (),
+        (),
+        (E.Oy3, E.Od3,),
         (),
         (),
     ),
     (1, 0): (
-        (E.Oy3, E.Ty, E.Tp, E.W0k, E.W0q,),
-        (E.On0, E.TF, E.Wk1, E.Tx, E.Sq, E.Wq1, E.On1, E.Sh0, E.Ox0, E.Sh1, E.Sk, E.Wk3, E.Od0, E.Oy0, E.Wk2, E.Oy1, E.On3, E.Pk, E.Wq3, E.Wq2, E.On2, E.Pq, E.Ox1,),
-        (E.Sh2, E.K1,),
+        (E.Wq3, E.Tp, E.On0, E.Ty, E.Wk3, E.Wk1, E.Ox0, E.W0k, E.Ox3, E.Sh0, E.On1, E.Oy3, E.TF, E.Tx, E.Od0, E.Sh1, E.On2, E.Sh2, E.Wq1, E.W0q, E.Wk2, E.Oy1,),
+        (),
+        (E.Sk, E.Sq, E.Ox2,),
+        (E.Wq2, E.On3, E.Oy0, E.K1, E.Sh3, E.Od3,),
+        (),
+        (E.K2,),
+        (E.Oy2, E.Od2,),
+        (E.Kp, E.Ox1,),
+        (),
+        (),
+        (),
         (E.Od1,),
-        (E.Od3, E.K2, E.Kp,),
-        (),
-        (E.Oy2, E.Ox2,),
-        (E.Od2, E.Sh3,),
-        (E.Ox3,),
+        (),
+        (),
+        (),
         (),
     ),
     (1, 1): (
-        (E.W0k, E.Ty, E.On0, E.Tp, E.Tx, E.Oy3, E.W0q, E.Od3, E.Sh0,),
-        (E.Sk, E.Wk1, E.On1, E.On3, E.TF, E.Wk3, E.Wk2, E.Sq,),
-        (E.Sh1, E.Wq1, E.Ox1, E.Pk, E.Wq2,),
-        (E.Oy1, E.Ox0, E.On2, E.Ox3, E.K2, E.Wq3, E.Pq, E.Sh2,),
-        (E.K1, E.Kp, E.Od1,),
-        (),
-        (E.Oy0, E.Ox2, E.Sh3, E.Oy2, E.Od0,),
-        (),
+        (E.On0, E.Wk3, E.W0k, E.Tp, E.Ty, E.W0q, E.Tx, E.Sk, E.Wq3, E.Sq, E.Sh0, E.On1, E.TF, E.Sh1, E.Wk1, E.Wq1,),
+        (E.K2, E.Wk2,),
+        (),
+        (E.Ox3, E.On2, E.Od3, E.Oy3, E.Ox0, E.Sh2,),
+        (E.Oy0,),
+        (E.Ox1, E.Oy1, E.Wq2,),
+        (),
+        (E.Ox2,),
+        (),
+        (E.On3, E.K1, E.Kp, E.Oy2, E.Od1, E.Od0,),
         (E.Od2,),
+        (),
+        (),
+        (E.Sh3,),
+        (),
         (),
     ),
     (2, 0): (
-        (E.Oy3, E.Ty, E.Tp, E.W0k, E.On0, E.W0q, E.Ox3, E.Wk1, E.On3, E.TF, E.Tx, E.Sh0,),
-        (E.Sk, E.On1, E.Wk3, E.Wk2, E.Sh1, E.Wq2, E.Wq1, E.Oy0,),
-        (E.Oy1, E.On2, E.Ox1, E.Pk, E.Ox0, E.Sq,),
-        (E.Sh2, E.Wq3, E.Pq, E.K2, E.Od0,),
-        (E.K1, E.Kp, E.Od1, E.Od3, E.Oy2, E.Ox2,),
-        (E.Sh3,),
-        (),
-        (),
+        (E.Tp, E.W0k, E.On0, E.Wk3, E.Wq3, E.Ty, E.Sk, E.Oy3, E.TF, E.W0q, E.Tx, E.On1, E.Wk1, E.Sh0, E.Sq, E.On2, E.Sh2, E.Ox0,),
+        (E.Ox1, E.Wk2, E.Sh1, E.Wq2, E.Ox3,),
+        (E.On3,),
+        (),
+        (E.Ox2,),
+        (),
+        (E.Wq1,),
+        (E.K2,),
+        (E.Oy2,),
+        (E.Oy1, E.Oy0, E.Od1, E.Od0,),
+        (E.K1, E.Kp,),
         (E.Od2,),
         (),
+        (),
+        (),
+        (E.Od3, E.Sh3,),
     ),
     (2, 1): (
-        (E.Oy3, E.Ty, E.W0k, E.Tx, E.Tp, E.On0, E.Sh0, E.W0q, E.Sk, E.TF, E.Wk1, E.On1, E.Sh1,),
-        (E.Wk2, E.Ox0, E.On3, E.Wk3,),
-        (E.Sq, E.Wq1, E.Wq3, E.Pk, E.Wq2, E.Oy1, E.Pq,),
-        (E.Ox1, E.Od0, E.On2, E.K1,),
-        (E.Sh2, E.Oy0, E.K2, E.Kp, E.Od3,),
-        (E.Ox2, E.Od1, E.Od2, E.Ox3, E.Oy2,),
-        (),
-        (),
-        (),
-        (E.Sh3,),
+        (E.Oy3, E.Tp, E.On0, E.W0k, E.Ty, E.Wk3, E.Tx, E.W0q, E.On1, E.Sh0, E.TF, E.Sk, E.Sq, E.Sh1, E.Wk2, E.Wk1,),
+        (),
+        (E.Wq2, E.On2,),
+        (E.Wq1, E.Sh2,),
+        (E.Ox2,),
+        (),
+        (E.Ox3, E.Ox1, E.K1, E.On3, E.Ox0, E.Od3,),
+        (),
+        (E.Oy1, E.Od1, E.Wq3,),
+        (E.K2, E.Oy0, E.Oy2, E.Od2, E.Kp, E.Sh3, E.Od0,),
+        (),
+        (),
+        (),
+        (),
+        (),
+        (),
     ),
     (3, 0): (
-        (E.W0k, E.Tp, E.Wk1, E.On0,),
-        (E.Ty, E.Sh0, E.W0q, E.Tx, E.On1, E.TF, E.Sh1, E.On2,),
-        (E.Wq1, E.Wk3, E.Sh2, E.Wk2, E.Sq, E.Oy1, E.Oy0, E.Ox0, E.Ox1, E.Wq3, E.On3, E.Sk, E.Sh3, E.Ox2, E.Pk, E.K1,),
-        (E.Od0, E.Oy3, E.Wq2, E.Oy2, E.Pq, E.K2, E.Kp,),
-        (E.Od2,),
-        (E.Od1,),
-        (),
-        (E.Ox3,),
+        (E.Ty, E.Tp, E.On0, E.W0k, E.On1, E.On2, E.W0q, E.Sh0, E.TF, E.Ox0, E.Ox2, E.Wk2, E.Oy0, E.Tx, E.Sh2, E.Sh1, E.On3, E.Wk1, E.Wk3, E.Ox1, E.Wq3, E.Wq1, E.Sh3,),
+        (),
+        (E.Oy2, E.Od1, E.K1, E.Sk,),
+        (),
+        (E.Oy3, E.Sq,),
+        (E.Wq2, E.Od2, E.Od0, E.Ox3,),
+        (),
+        (),
+        (E.K2,),
+        (E.Kp,),
+        (E.Oy1,),
+        (),
+        (),
         (),
         (E.Od3,),
+        (),
     ),
     (3, 1): (
-        (),
-        (E.W0k, E.Ty, E.On0, E.Tp, E.Tx, E.W0q, E.Sh0, E.TF, E.On1, E.Wk2, E.Sk, E.On2, E.Sh1, E.Sq, E.Ox0, E.Wk1, E.Sh2, E.Oy2, E.Wk3, E.Pk, E.Ox1, E.Oy0, E.Wq2, E.Od0,),
-        (E.Oy1, E.Ox2, E.Wq1, E.Wq3,),
-        (E.On3, E.Pq, E.Sh3, E.K1,),
-        (E.K2, E.Kp, E.Od1, E.Od2,),
-        (E.Oy3, E.Ox3, E.Od3,),
+        (E.Ty, E.On0, E.Tp, E.W0q, E.Sh0, E.Sq, E.W0k, E.Tx, E.On1, E.On2, E.Sh2, E.Sk, E.Oy0, E.Sh1, E.TF, E.Ox0, E.Wk3, E.Wk1, E.Ox2,),
+        (),
+        (),
+        (E.Oy1, E.Ox3,),
+        (E.On3, E.Od0, E.Wq3, E.Sh3, E.Wk2, E.Wq2,),
+        (E.Wq1,),
+        (E.Oy3, E.Oy2, E.K2,),
+        (E.K1,),
+        (E.Od2, E.Ox1,),
+        (),
+        (E.Kp,),
+        (E.Od1, E.Od3,),
         (),
         (),
         (),
@@ -335,7 +381,7 @@
         b = 2 * zz + self.c
         where = ((self.me + 2, self.head), (self.me - 2, self.head), self.partner)[way]
         ref = self.w_ref(b, part)
-        return self.remote(ref, ref, e.w_send, e.w_recv.at[part, LINE if way == 2 else zz], where)
+        return self.remote(ref, ref, e.w_send, e.w_recv.at[part, LINE + zz if way == 2 else zz], where)
 
     def w_onward(self, part, zz):
         return [
@@ -356,8 +402,9 @@
     def w_take(self, part, zz):
         self.remote_take(self.w_ref(2 * zz + self.c, part), self.e.w_recv.at[part, zz])
 
-    def w_beside(self, part):
-        self.remote_take(self.units(LINE), self.e.w_recv.at[part, LINE])
+    def w_beside(self, part, k):
+        for zz in sides(self.z, k):
+            self.remote_take(self.units(1), self.e.w_recv.at[part, LINE + zz])
 
     def units(self, n):
         return self.e.WO.at[pl.ds(0, n * self.e.deep)]
@@ -458,18 +505,28 @@
         where = (
             self.partner, self.yn, self.xn, (2 * self.z + 1 - self.x, 2 * (1 - self.y) + self.c),
         )[way]
-        return self.remote(e.AO, e.ATT.at[self.hg], e.a_send, e.a_recv.at[0 if way == 0 else self.hg], where)
+        return self.remote(e.AO, e.ATT.at[self.hg], e.a_send, e.a_recv.at[self.hg], where)
 
     def a_ways(self):
         return (1, 0) if self.kind == 0 else (2, 3)
 
     def a_pass(self, h):
         e = self.e
-        return self.remote(e.ATT.at[h], e.ATT.at[h], e.a_send, e.a_recv.at[0], self.partner)
-
-    def a_far(self):
+        return self.remote(e.ATT.at[h], e.ATT.at[h], e.a_send, e.a_recv.at[h], self.partner)
+
+    def a_order(self):
         x, y = self.x, self.y
-        return (2 * (1 - y) + x, 2 * y + 1 - x, 2 * (1 - y) + 1 - x)
+        return (2 * y + x, 2 * (1 - y) + x, 2 * y + 1 - x, 2 * (1 - y) + 1 - x)
+
+    def tell(self, zz):
+        e = self.e
+        if (self.z, self.kind, zz) in e.loaded:
+            return
+        e.loaded.add((self.z, self.kind, zz))
+        for px in range(2):
+            self.remote(
+                e.SEG.at[self.me], e.SEG.at[self.me], e.s_send, e.s_recv, (2 * zz + px, self.head)
+            ).start()
 
     def do(self, event):
         z, kind, e = self.z, self.kind, self.e
@@ -490,9 +547,8 @@
             part = "qk".index(name[1])
             for zz in sides(z, int(k)):
                 self.w_take(part, zz)
+                self.tell(zz)
                 begin(self.w_onward(part, zz))
-        elif name == "P":
-            self.w_beside("qk".index(k))
         elif event in ("Tp", "Tx", "Ty"):
             if (z, kind) not in e.loaded:
                 e.loaded.add((z, kind))
@@ -508,6 +564,7 @@
                 for i in range(PIECES):
                     if zz != z:
                         self.o_take(zz, 0, 0, i)
+                        self.tell(zz)
                     elif i == 0:
                         e.l_out.wait()
                     begin(self.o_onward(zz, i))
@@ -551,14 +608,14 @@
         for way in self.a_ways():
             self.a_copy(way).start()
 
-    def gathered(self):
-        e = self.e
-        if self.kind == 0:
-            for h in self.a_far():
-                self.remote_take(e.ATT.at[h], e.a_recv.at[h])
-                self.a_pass(h).start()
-        else:
-            self.remote_take(e.ATT, e.a_recv.at[0])
+    def gathered(self, i):
+        e = self.e
+        h = self.a_order()[i]
+        if self.kind == 1 or i > 0:
+            self.remote_take(e.ATT.at[h], e.a_recv.at[h])
+        if self.kind == 0 and i > 0:
+            self.a_pass(h).start()
+        if self.kind == 1 and i == 3:
             self.remote_take(e.X.at[1], e.r_recv)
 
     def emitted(self, k):
@@ -567,15 +624,12 @@
 
     def drain(self):
         z, kind, e = self.z, self.kind, self.e
-        weights = sum(len(self.w_onward(part, zz)) for part in range(2) for zz in range(LINE))
-        self.remote_left(self.units(weights + 2 * kind), e.w_send)
-        outs = sum(
-            len(self.o_onward(zz, 0)) + 2 + len(self.o_from_x(zz, 0)) + len(self.o_from_y(zz, 0)) - 2
-            for zz in range(LINE)
-        )
-        self.remote_left(self.units(outs), e.o_send)
+        onward = 1 if z in (0, LINE - 1) else LINE + 1
+        self.remote_left(self.units(2 * (onward + LINE + kind)), e.w_send)
+        self.remote_left(self.units(onward + 3 * LINE), e.o_send)
         self.remote_left(self.units(4 * LINE), e.oc_send)
-        keys = sum(len(self.k_onward(zz)) for zz in range(max(z - REACH, 0), z + 1))
+        held = z + 1 - max(z - REACH, 0)
+        keys = held + (min(z + 1, REACH) if z < LINE - 1 else 0)
         self.remote_left(e.KV.at[pl.ds(0, keys)], e.k_send)
         self.remote_left(e.X.at[0, pl.ds(0, 3 + kind)], e.t_send)
         self.remote_left(e.KV.at[pl.ds(0, 2 if kind else 5)], e.a_send)
@@ -591,7 +645,7 @@
     seq, heads, rows, width, most,
     tok, seg_row, wq, wk, wv, wo_in, pre_in, post_in, freq_in,
     out,
-    TOK, X, XN, SW, W, WO, SEG, KV, AO, ATT, PR, RQ, NUM, DEN, pre1, post1, pre, post, freq,
+    TOK, X, XN, SW, W, WO, SEG, KV, AO, ATT, PR, ACC, RQ, NUM, DEN, pre1, post1, pre, post, freq,
     loc, t_recv, t_send, r_recv, r_send, s_recv, s_send, w_recv, w_send,
     o_recv, o_side, o_send, oc_send, k_recv, k_send, a_recv, a_send,
 ):
@@ -612,7 +666,7 @@
     e.TOK, e.X, e.SW, e.W, e.WO, e.KV, e.AO, e.ATT = TOK, X, SW, W, WO, KV, AO, ATT
     e.t_recv, e.t_send, e.r_recv, e.r_send = t_recv, t_send, r_recv, r_send
     e.w_recv, e.w_send, e.o_recv, e.o_side = w_recv, w_send, o_recv, o_side
-    e.o_send, e.oc_send = o_send, oc_send
+    e.o_send, e.oc_send, e.SEG, e.s_recv, e.s_send = o_send, oc_send, SEG, s_recv, s_send
     e.k_recv, e.k_send, e.a_recv, e.a_send = k_recv, k_send, a_recv, a_send
 
     def load_weights(block):
@@ -663,20 +717,22 @@
     for dx in range(2):
         for dy in range(2):
             for dc in range(2):
-                if dy + dc > 0:
+                if dx + dy + dc > 0:
                     gx = lax.rem(x + dx, 2)
                     greet((2 * z + gx, 2 * lax.rem(y + dy, 2) + lax.rem(c + dc, 2)))
-    for d in range(1, seq):
-        greet((lax.rem(me + d, seq), head))
-    pl.semaphore_wait(barrier, 6 + seq - 1)
+
+    @pl.when(z > 0)
+    def _():
+        greet((me - 2, head))
+
+    @pl.when(z < LINE - 1)
+    def _():
+        greet((me + 2, head))
+
+    ends = (z > 0).astype(jnp.int32) + (z < LINE - 1).astype(jnp.int32)
+    pl.semaphore_wait(barrier, 7 + ends)
 
     l_seg.wait()
-
-    def s_copy(d):
-        return pltpu.make_async_remote_copy(
-            src_ref=SEG.at[me], dst_ref=SEG.at[me], send_sem=s_send, recv_sem=s_recv,
-            device_id=(lax.rem(me + d, seq), head), device_id_type=MESH,
-        )
 
     def s_all():
         ref = SEG.at[pl.ds(0, seq - 1)]
@@ -685,8 +741,10 @@
             device_id=(lax.rem(me + 1, seq), head), device_id_type=MESH,
         )
 
-    for d in range(1, seq):
-        s_copy(d).start()
+    pltpu.make_async_remote_copy(
+        src_ref=SEG.at[me], dst_ref=SEG.at[me], send_sem=s_send, recv_sem=s_recv,
+        device_id=(2 * z + 1 - x, head), device_id_type=MESH,
+    ).start()
 
     def everyone(act):
         for place in range(LINE):
@@ -695,6 +753,19 @@
                 def _():
                     act(Moves(place, kind, e))
 
+    def around(k, act):
+        if k == 0:
+            act(z)
+        else:
+
+            @pl.when(z >= k)
+            def _():
+                act(z - k)
+
+            @pl.when(z + k < LINE)
+            def _():
+                act(z + k)
+
     def events(phase):
         def act(moves):
             for event in PLAN[moves.z, moves.kind][phase]:
@@ -703,13 +774,31 @@
         everyone(act)
 
     events(0)
-    s_all().wait_recv()
     for move in small:
         move.wait()
     for h in range(heads):
         at = slice(h * cut, (h + 1) * cut)
         pre[0:1, at] = pre1[at][None, :]
         post[0:1, at] = post1[at][None, :]
+    everyone(lambda moves: moves.tokens())
+    half = rows // 2
+
+    def norm_rows(r, _):
+        at = pl.ds(pl.multiple_of(r * half, half), half)
+        total = jnp.zeros((half, 1), F32)
+        for h in range(heads):
+            wide = X[0, h, at, :].astype(F32)
+            total += jnp.sum(wide * wide, axis=1, keepdims=True)
+        scale = lax.rsqrt(total / width + EPS)
+        for h in range(heads):
+            gain = pre[0:1, h * cut : (h + 1) * cut]
+            XN[h, at, :] = (X[0, h, at, :].astype(F32) * scale * gain).astype(BF16)
+        return 0
+
+    lax.fori_loop(0, 2, norm_rows, 0)
+
+    events(1)
+    s_all().wait_recv()
     own = jnp.broadcast_to(SEG[rb].astype(F32), (HD, rows))
     col = jnp.transpose(own)[:, 0:1]
     start = jnp.zeros((rows, 1), F32)
@@ -722,48 +811,35 @@
     lane = lax.broadcasted_iota(jnp.int32, (rows, HD), 1)
     sine = jnp.where(lane < HD // 2, -sine, sine)
 
-    events(1)
-    everyone(lambda moves: moves.tokens())
-    half = rows // 2
-
-    def norm_rows(r, _):
-        at = pl.ds(pl.multiple_of(r * half, half), half)
-        total = jnp.zeros((half, 1), F32)
-        for h in range(heads):
-            wide = X[0, h, at, :].astype(F32)
-            total += jnp.sum(wide * wide, axis=1, keepdims=True)
-        scale = lax.rsqrt(total / width + EPS)
-        for h in range(heads):
-            gain = pre[0:1, h * cut : (h + 1) * cut]
-            XN[h, at, :] = (X[0, h, at, :].astype(F32) * scale * gain).astype(BF16)
-        return 0
-
-    lax.fori_loop(0, 2, norm_rows, 0)
-
-    def project(part):
+    def project(part, k):
         cols = slice(part * qd, (part + 1) * qd)
-        total = jnp.zeros((rows, qd), F32)
-        for h in range(heads):
-            some = slice(h * cut, (h + 1) * cut)
-            total += jnp.dot(XN[h], W[some, cols], preferred_element_type=F32)
-        return total
+        everyone(lambda moves: moves.w_beside(part, k))
+
+        def add(n):
+            some = pl.ds(pl.multiple_of(n * cut, 128), cut)
+            value = jnp.dot(XN[n], W[some, cols], preferred_element_type=F32)
+            ACC[:, cols] = value if k == 0 else ACC[:, cols] + value
+
+        around(k, add)
 
     def turn(values):
         return values * cosine + pltpu.roll(values, HD // 2, 1) * sine
 
-    events(2)
-    keyed = project(1)
-    KV[rb, :, 0:HD] = turn(keyed[:, 0:HD]).astype(BF16)
-    KV[rb, :, HD : 2 * HD] = keyed[:, kd : kd + HD].astype(BF16)
+    for k in range(LINE):
+        events(2 + k)
+        project(1, k)
+    KV[rb, :, 0:HD] = turn(ACC[:, qd : qd + HD]).astype(BF16)
+    KV[rb, :, HD : 2 * HD] = ACC[:, qd + kd : qd + kd + HD].astype(BF16)
     everyone(lambda moves: [copy.start() for copy in moves.k_onward(moves.z)])
-    events(3)
-    asked = project(0)
+    for k in range(LINE):
+        events(2 + LINE + k)
+        project(0, k)
     for g in range(GROUP):
         RQ[g * rows : (g + 1) * rows, :] = (
-            turn(asked[:, g * HD : (g + 1) * HD]) * SCALAR ** (-0.5)
+            turn(ACC[:, g * HD : (g + 1) * HD]) * SCALAR ** (-0.5)
         ).astype(BF16)
 
-    events(4)
+    events(2 + 2 * LINE)
     start2 = jnp.concatenate([start] * GROUP, axis=0)
     index2 = jnp.concatenate([index] * GROUP, axis=0)
     NUM[...] = jnp.zeros_like(NUM)
@@ -792,35 +868,33 @@
         for g in range(GROUP):
             ATT[hg, :, g * HD : (g + 1) * HD] = ratio[g * rows : (g + 1) * rows, :]
 
-    events(5)
-    everyone(lambda moves: moves.gathered())
-
-    def emit(n):
-        acc = jnp.zeros((rows, cut), F32)
-        for h in range(heads):
-            acc += lax.dot_general(
-                ATT[h], WO[pl.ds(pl.multiple_of(h * width + n * cut, 128), cut), :],
-                (((1,), (1,)), ((), ())), preferred_element_type=F32,
-            )
-        PR[n] = acc
-        DEN[0:rows, 0:1] += jnp.sum(acc * acc, axis=1, keepdims=True)
-
-    DEN[...] = jnp.zeros_like(DEN)
-    for k in range(LINE):
-        events(6 + k)
-        everyone(lambda moves: moves.emitted(k))
-        if k == 0:
-            emit(z)
-        else:
-
-            @pl.when(z >= k)
-            def _():
-                emit(z - k)
-
-            @pl.when(z + k < LINE)
-            def _():
-                emit(z + k)
-    scale = lax.rsqrt(DEN[0:rows, 0:1] / width + EPS)
+    def emit(i, n):
+        acc = lax.dot_general(
+            ATT[order[i]], WO[pl.ds(pl.multiple_of(order[i] * width + n * cut, 128), cut), :],
+            (((1,), (1,)), ((), ())), preferred_element_type=F32,
+        )
+        PR[n] = acc if i == 0 else PR[n] + acc
+
+    order = (hg, 2 * (1 - y) + x, 2 * y + 1 - x, 2 * (1 - y) + 1 - x)
+    for i in range(heads):
+        events(3 + 2 * LINE + i)
+        everyone(lambda moves: moves.gathered(i))
+        for k in range(LINE - 1):
+            if i == 0:
+                everyone(lambda moves: moves.emitted(k))
+            around(k, functools.partial(emit, i))
+    events(3 + 2 * LINE + heads)
+    everyone(lambda moves: moves.emitted(LINE - 1))
+
+    def emit_all(n):
+        for i in range(heads):
+            emit(i, n)
+
+    around(LINE - 1, emit_all)
+    squares = jnp.zeros((rows, 1), F32)
+    for h in range(heads):
+        squares += jnp.sum(PR[h] * PR[h], axis=1, keepdims=True)
+    scale = lax.rsqrt(squares / width + EPS)
     kept = other.astype(jnp.int32)
 
     def finish(h, _):
@@ -863,6 +937,7 @@
             pltpu.VMEM((rows, GROUP * HD), BF16),
             pltpu.VMEM((heads, rows, GROUP * HD), BF16),
             pltpu.VMEM((heads, rows, cut), F32),
+            pltpu.VMEM((rows, qd + 2 * kd), F32),
             pltpu.VMEM((GROUP * rows, HD), BF16),
             pltpu.VMEM((GROUP * rows, HD), F32),
             pltpu.VMEM((GROUP * rows, HD), F32),
@@ -873,7 +948,7 @@
             pltpu.VMEM((1, HD), F32),
             dma((10,)),
             dma((heads,)), dma, dma, dma, dma, dma,
-            dma((2, LINE + 1)), dma,
+            dma((2, 2 * LINE)), dma,
             dma((4, LINE, PIECES)), dma((LINE,)), dma, dma,
             dma((LINE + 1,)), dma, dma((heads,)), dma,
         ],

time: 88.2 us -> 86.4 us (0.980)
  Pallas kernels: 86.6 us -> 84.7 us
    pallas_call x1, Pallas kernels: 86.6 us -> 84.7 us  [fused(): pl.pallas_call(functools.partial(kernel, seq, heads, rows, width, most),...]
where the time goes in v3:
time: 86.4 us; the launch traced here: 86.1 us
  Pallas kernels  84.7 us (98%)
  local copies, waits for them, and re-layouts  1.41 us (2%)
    pallas_call x1, Pallas kernels, fused(): pl.pallas_call(functools.partial(kernel, seq, heads, rows, width, most),...  84.7 us

profile of v3, /device:TPU:29, one launch (start us, length us, event | category | flops | bytes accessed | tf_op | source)
XLA Modules:
  0.0 86.1 jit_solution(2885758296069960358)
XLA Ops:
  0.0 84.7 %shard_map.91 = bf16[256,4608]{1,0:T(8,128)(2,1)S(1)} custom-call(bf16[256,1152]{1,0:T(8,128)(2,1)} %tok.1, s32[1,256]{1,0:T(1,128)} %bitcast.3, bf16[576,256]{1,0:T(8,128)(2,1)} %wq.1, bf16[576,128]{1,0:T(8,128)(2,1)} %wk.1, bf16[576,128]{1,0:T(8,128)(2,1)} %wv.1, bf16[576,256]{1,0:T(8,128)(2,1)} %bitcast.2, f32[4608]{0:T(1024)} %pre_in.1, f32[4608]{0:T(1024)} %post_in.1, ...), custom_call_target="tpu_custom_call" | custom-call | tf_op jit(solution)/shard_map/pallas_call | solution.py:923
  84.7 1.4 %copy.11 = bf16[256,4608]{1,0:T(8,128)(2,1)} copy(bf16[256,4608]{1,0:T(8,128)(2,1)S(1)} %shard_map.91) | data formatting | bytes 4718592

commit v4 on v3

--- a/solution.py
+++ b/solution.py
@@ -141,6 +141,7 @@
 F32 = jnp.float32
 LINE = 4
 REACH = LINE // 2
+LOG2E = 1.4426950408889634
 PIECES = 1
 OVER_X = (0,)
 
@@ -186,145 +187,145 @@
 
 PLAN = {
     (0, 0): (
-        (E.On0, E.Tp, E.Ty, E.Tx, E.W0q, E.W0k, E.On1, E.Sh1, E.On2, E.TF, E.Sh0, E.Ox1, E.Wk1,),
-        (E.Sk, E.Wq1, E.On3, E.Sh2,),
-        (E.Wk2, E.Sh3, E.Sq, E.Wk3,),
-        (),
-        (),
-        (),
-        (E.Oy0, E.Ox2, E.Wq2, E.Wq3,),
-        (E.K1, E.Od1, E.K2, E.Ox0, E.Od0,),
-        (),
-        (),
-        (E.Oy1, E.Od2, E.Kp,),
-        (E.Oy2, E.Oy3,),
-        (E.Ox3,),
+        (E.Ty, E.Tp, E.W0q, E.On0, E.W0k, E.Sh0, E.On1, E.Tx, E.On2, E.K2, E.Sk, E.Wk1, E.Sh2, E.TF, E.On3, E.Sh3, E.Sh1, E.Oy3, E.Ox2,),
+        (E.Ox0, E.Wk3, E.Ox1, E.Wq1, E.Wk2,),
+        (),
+        (),
+        (),
+        (E.Oy2,),
+        (E.Wq2, E.Sq, E.Oy0, E.Ox3, E.Wq3, E.K1,),
+        (E.Oy1, E.Od1,),
+        (),
+        (E.Od2,),
+        (E.Od0, E.Kp,),
         (),
         (E.Od3,),
+        (),
+        (),
         (),
     ),
     (0, 1): (
-        (E.On0, E.Tp, E.W0k, E.Ty, E.W0q, E.Sq, E.Sh0, E.On2, E.Sk, E.Wq1, E.Tx, E.On1, E.Ox1, E.Sh1, E.Oy1, E.TF, E.Sh2, E.Wk1, E.Wk3, E.Ox2, E.Oy0,),
-        (E.Wk2, E.Oy2,),
-        (E.Wq2,),
-        (),
-        (E.On3, E.Od1,),
-        (E.Od2, E.Ox0, E.K2, E.K1, E.Wq3,),
-        (),
-        (E.Ox3,),
-        (E.Od0, E.Sh3,),
-        (E.Kp,),
-        (),
-        (),
-        (),
-        (E.Oy3, E.Od3,),
+        (E.On0, E.Ty, E.W0k, E.Tx, E.W0q, E.Sk, E.Sh0, E.Tp, E.TF, E.On1, E.Sq, E.On2, E.Wq1, E.Wk1, E.Sh1, E.Sh2,),
+        (E.Wk2, E.Ox2,),
+        (E.Wk3,),
+        (E.Oy2, E.Ox3, E.On3, E.Wq2, E.Sh3, E.Oy0,),
+        (E.K2,),
+        (),
+        (E.Ox1,),
+        (E.Od2, E.Wq3, E.Od3,),
+        (E.K1, E.Oy3,),
+        (),
+        (E.Oy1, E.Ox0, E.Od1, E.Kp, E.Od0,),
+        (),
+        (),
+        (),
         (),
         (),
     ),
     (1, 0): (
-        (E.Wq3, E.Tp, E.On0, E.Ty, E.Wk3, E.Wk1, E.Ox0, E.W0k, E.Ox3, E.Sh0, E.On1, E.Oy3, E.TF, E.Tx, E.Od0, E.Sh1, E.On2, E.Sh2, E.Wq1, E.W0q, E.Wk2, E.Oy1,),
-        (),
-        (E.Sk, E.Sq, E.Ox2,),
-        (E.Wq2, E.On3, E.Oy0, E.K1, E.Sh3, E.Od3,),
-        (),
+        (E.Ty, E.Tp, E.On0, E.W0k, E.TF, E.Tx, E.Wk1, E.On1, E.Sh0,),
+        (E.Wq3, E.Sk, E.Wk3, E.On2, E.Wq1, E.Sh2, E.W0q, E.Od3, E.Sh1, E.Ox0, E.Wk2, E.Od0, E.On3, E.Ox2,),
+        (E.Oy1,),
+        (E.K1, E.Sq, E.Oy2, E.Wq2,),
+        (),
+        (E.Ox1,),
+        (E.Oy0,),
+        (),
+        (E.Od2,),
         (E.K2,),
-        (E.Oy2, E.Od2,),
-        (E.Kp, E.Ox1,),
-        (),
-        (),
-        (),
-        (E.Od1,),
-        (),
-        (),
-        (),
-        (),
+        (E.Kp, E.Od1, E.Ox3,),
+        (),
+        (E.Oy3,),
+        (),
+        (),
+        (E.Sh3,),
     ),
     (1, 1): (
-        (E.On0, E.Wk3, E.W0k, E.Tp, E.Ty, E.W0q, E.Tx, E.Sk, E.Wq3, E.Sq, E.Sh0, E.On1, E.TF, E.Sh1, E.Wk1, E.Wq1,),
-        (E.K2, E.Wk2,),
-        (),
-        (E.Ox3, E.On2, E.Od3, E.Oy3, E.Ox0, E.Sh2,),
-        (E.Oy0,),
-        (E.Ox1, E.Oy1, E.Wq2,),
-        (),
-        (E.Ox2,),
-        (),
-        (E.On3, E.K1, E.Kp, E.Oy2, E.Od1, E.Od0,),
+        (E.On0, E.Ty, E.W0k, E.W0q, E.Tx, E.Sk, E.Sh0, E.K2, E.Tp, E.On1, E.On3, E.TF, E.Sq, E.Sh1, E.Ox3, E.Wk1,),
+        (E.On2, E.Wk3, E.Ox0,),
+        (E.Wk2, E.Wq1, E.Sh2,),
+        (E.Od0,),
+        (),
+        (),
+        (E.Ox1, E.Oy2, E.Wq2, E.K1, E.Oy3,),
+        (E.Kp, E.Oy0, E.Sh3, E.Oy1,),
+        (E.Wq3, E.Od1, E.Ox2, E.Od3,),
+        (),
+        (),
         (E.Od2,),
         (),
         (),
-        (E.Sh3,),
         (),
         (),
     ),
     (2, 0): (
-        (E.Tp, E.W0k, E.On0, E.Wk3, E.Wq3, E.Ty, E.Sk, E.Oy3, E.TF, E.W0q, E.Tx, E.On1, E.Wk1, E.Sh0, E.Sq, E.On2, E.Sh2, E.Ox0,),
-        (E.Ox1, E.Wk2, E.Sh1, E.Wq2, E.Ox3,),
-        (E.On3,),
-        (),
-        (E.Ox2,),
-        (),
-        (E.Wq1,),
-        (E.K2,),
-        (E.Oy2,),
-        (E.Oy1, E.Oy0, E.Od1, E.Od0,),
-        (E.K1, E.Kp,),
-        (E.Od2,),
-        (),
-        (),
-        (),
-        (E.Od3, E.Sh3,),
+        (E.Ty, E.Tp, E.W0k, E.W0q, E.On0, E.Sk, E.TF, E.Tx, E.Wk3, E.On1, E.Wk1, E.Od3, E.Ox0,),
+        (E.Sh0, E.On2, E.Sq, E.Wk2, E.Wq2,),
+        (),
+        (E.Sh2, E.Sh1,),
+        (E.Ox3, E.Ox2, E.Wq1, E.Ox1, E.Oy3, E.K2, E.Oy2, E.Od0, E.Oy0,),
+        (E.Oy1,),
+        (E.Wq3, E.On3, E.K1, E.Od2, E.Od1,),
+        (),
+        (E.Sh3,),
+        (),
+        (E.Kp,),
+        (),
+        (),
+        (),
+        (),
+        (),
     ),
     (2, 1): (
-        (E.Oy3, E.Tp, E.On0, E.W0k, E.Ty, E.Wk3, E.Tx, E.W0q, E.On1, E.Sh0, E.TF, E.Sk, E.Sq, E.Sh1, E.Wk2, E.Wk1,),
-        (),
-        (E.Wq2, E.On2,),
-        (E.Wq1, E.Sh2,),
-        (E.Ox2,),
-        (),
-        (E.Ox3, E.Ox1, E.K1, E.On3, E.Ox0, E.Od3,),
-        (),
-        (E.Oy1, E.Od1, E.Wq3,),
-        (E.K2, E.Oy0, E.Oy2, E.Od2, E.Kp, E.Sh3, E.Od0,),
-        (),
-        (),
+        (E.Ty, E.On0, E.W0k, E.Sh0, E.W0q, E.On1, E.Tx, E.Sk, E.Tp, E.Sh1, E.Wk1, E.TF, E.Wk2, E.Sq,),
+        (E.Od3, E.Ox3, E.On3, E.On2,),
+        (E.Sh2,),
+        (E.Oy0,),
+        (),
+        (E.Wq1, E.Wq2, E.Wk3,),
+        (),
+        (E.Ox1,),
+        (),
+        (E.K1, E.Wq3, E.Ox2,),
+        (E.Sh3, E.Oy1, E.Oy2, E.Ox0, E.K2, E.Kp, E.Od1,),
+        (E.Oy3, E.Od0, E.Od2,),
         (),
         (),
         (),
         (),
     ),
     (3, 0): (
-        (E.Ty, E.Tp, E.On0, E.W0k, E.On1, E.On2, E.W0q, E.Sh0, E.TF, E.Ox0, E.Ox2, E.Wk2, E.Oy0, E.Tx, E.Sh2, E.Sh1, E.On3, E.Wk1, E.Wk3, E.Ox1, E.Wq3, E.Wq1, E.Sh3,),
-        (),
-        (E.Oy2, E.Od1, E.K1, E.Sk,),
-        (),
-        (E.Oy3, E.Sq,),
-        (E.Wq2, E.Od2, E.Od0, E.Ox3,),
-        (),
-        (),
-        (E.K2,),
-        (E.Kp,),
-        (E.Oy1,),
-        (),
-        (),
-        (),
-        (E.Od3,),
+        (E.Ty, E.Tp, E.W0q, E.On0, E.W0k, E.On1, E.TF, E.On2, E.Sh0, E.Wk1, E.Wq1, E.Tx, E.Sk, E.Ox2, E.Ox0, E.Sh1, E.On3, E.Ox1, E.Sh2, E.Wk2, E.Od1,),
+        (E.Sh3, E.Wq2,),
+        (),
+        (E.Oy0, E.Sq, E.Wk3,),
+        (),
+        (E.Od2, E.Oy2,),
+        (E.Ox3, E.Oy3,),
+        (),
+        (E.Wq3,),
+        (E.K1, E.K2,),
+        (E.Oy1, E.Kp,),
+        (E.Od3, E.Od0,),
+        (),
+        (),
+        (),
         (),
     ),
     (3, 1): (
-        (E.Ty, E.On0, E.Tp, E.W0q, E.Sh0, E.Sq, E.W0k, E.Tx, E.On1, E.On2, E.Sh2, E.Sk, E.Oy0, E.Sh1, E.TF, E.Ox0, E.Wk3, E.Wk1, E.Ox2,),
-        (),
-        (),
-        (E.Oy1, E.Ox3,),
-        (E.On3, E.Od0, E.Wq3, E.Sh3, E.Wk2, E.Wq2,),
-        (E.Wq1,),
-        (E.Oy3, E.Oy2, E.K2,),
-        (E.K1,),
-        (E.Od2, E.Ox1,),
-        (),
-        (E.Kp,),
-        (E.Od1, E.Od3,),
-        (),
+        (E.Ty, E.W0k, E.On0, E.W0q, E.Tx, E.On1, E.Sh0, E.Sk, E.On2, E.Tp, E.TF, E.Sh2, E.Sq,),
+        (E.Sh1, E.Wk1, E.Ox0, E.Oy2, E.Wk3, E.On3,),
+        (E.Ox2,),
+        (E.Wk2, E.Sh3, E.Wq1, E.Od2,),
+        (E.Wq2,),
+        (E.Oy1, E.K1,),
+        (E.Ox1,),
+        (E.Ox3, E.Wq3,),
+        (),
+        (E.K2,),
+        (E.Od0, E.Oy3, E.Oy0, E.Kp,),
+        (E.Od1,),
+        (E.Od3,),
         (),
         (),
         (),
@@ -840,25 +841,30 @@
         ).astype(BF16)
 
     events(2 + 2 * LINE)
+    NUM[...] = jnp.zeros_like(NUM)
+    DEN[...] = jnp.zeros_like(DEN)
+
     start2 = jnp.concatenate([start] * GROUP, axis=0)
     index2 = jnp.concatenate([index] * GROUP, axis=0)
-    NUM[...] = jnp.zeros_like(NUM)
-    DEN[...] = jnp.zeros_like(DEN)
-
-    def attend(j, _):
+
+    def attend(j, last):
         s = lax.dot_general(
             RQ[...], KV[j, :, 0:HD], (((1,), (1,)), ((), ())), preferred_element_type=F32
         )
         at = (j * rows + lax.broadcasted_iota(jnp.int32, (1, rows), 1)).astype(F32)
-        p = jnp.where(
-            (at >= start2) & (at <= index2), jnp.exp(CAP * jnp.tanh(s * (1.0 / CAP))), 0.0
-        )
-        DEN[...] += jnp.sum(p, axis=1, keepdims=True)
+        allowed = at >= start2
+        if last:
+            allowed = allowed & (at <= index2)
+        p = jnp.where(allowed, jnp.exp2((CAP * LOG2E) * jnp.tanh(s * (1.0 / CAP))), 0.0)
+        DEN[...] += sum(p[:, k : k + HD] for k in range(0, rows, HD))
         NUM[...] += jnp.dot(p.astype(BF16), KV[j, :, HD : 2 * HD], preferred_element_type=F32)
         return 0
 
-    lax.fori_loop(jnp.maximum(rb - most // rows, 0), rb + 1, attend, 0)
-    ratio = (NUM[...] / DEN[:, 0:1]).astype(BF16)
+    lax.fori_loop(
+        jnp.maximum(rb - most // rows, 0), rb, lambda j, _: attend(j, False), 0
+    )
+    attend(rb, True)
+    ratio = (NUM[...] / jnp.sum(DEN[...], axis=1, keepdims=True)).astype(BF16)
     for g in range(GROUP):
         AO[:, g * HD : (g + 1) * HD] = ratio[g * rows : (g + 1) * rows, :]
     everyone(lambda moves: moves.attended())

time: 86.4 us -> 83.8 us (0.970)
  Pallas kernels: 84.7 us -> 81.6 us
    pallas_call x1, Pallas kernels: 84.7 us -> 81.6 us  [fused(): pl.pallas_call(functools.partial(kernel, seq, heads, rows, width, most),...]
where the time goes in v4:
time: 83.8 us; the launch traced here: 83 us
  Pallas kernels  81.6 us (97%)
  local copies, waits for them, and re-layouts  1.41 us (2%)
    pallas_call x1, Pallas kernels, fused(): pl.pallas_call(functools.partial(kernel, seq, heads, rows, width, most),...  81.6 us

profile of v4, /device:TPU:29, one launch (start us, length us, event | category | flops | bytes accessed | tf_op | source)
XLA Modules:
  0.0 83.0 jit_solution(2792647312578304882)
XLA Ops:
  0.0 81.6 %shard_map.91 = bf16[256,4608]{1,0:T(8,128)(2,1)S(1)} custom-call(bf16[256,1152]{1,0:T(8,128)(2,1)} %tok.1, s32[1,256]{1,0:T(1,128)} %bitcast.3, bf16[576,256]{1,0:T(8,128)(2,1)} %wq.1, bf16[576,128]{1,0:T(8,128)(2,1)} %wk.1, bf16[576,128]{1,0:T(8,128)(2,1)} %wv.1, bf16[576,256]{1,0:T(8,128)(2,1)} %bitcast.2, f32[4608]{0:T(1024)} %pre_in.1, f32[4608]{0:T(1024)} %post_in.1, ...), custom_call_target="tpu_custom_call" | custom-call | tf_op jit(solution)/shard_map/pallas_call | solution.py:929
  81.6 1.4 %copy.11 = bf16[256,4608]{1,0:T(8,128)(2,1)} copy(bf16[256,4608]{1,0:T(8,128)(2,1)S(1)} %shard_map.91) | data formatting | bytes 4718592

commit v5 on v4

--- a/solution.py
+++ b/solution.py
@@ -187,35 +187,35 @@
 
 PLAN = {
     (0, 0): (
-        (E.Ty, E.Tp, E.W0q, E.On0, E.W0k, E.Sh0, E.On1, E.Tx, E.On2, E.K2, E.Sk, E.Wk1, E.Sh2, E.TF, E.On3, E.Sh3, E.Sh1, E.Oy3, E.Ox2,),
-        (E.Ox0, E.Wk3, E.Ox1, E.Wq1, E.Wk2,),
-        (),
-        (),
-        (),
+        (E.On0, E.W0q, E.Sh0, E.W0k, E.Ty, E.On1, E.K2, E.On2, E.Sk, E.Tp, E.Tx, E.Sh2, E.Wk1, E.TF, E.On3, E.Sh3, E.Sh1, E.Ox0,),
+        (E.Oy3, E.Ox2, E.Wk3, E.Ox1, E.Wk2,),
+        (),
+        (E.Wq1,),
         (E.Oy2,),
-        (E.Wq2, E.Sq, E.Oy0, E.Ox3, E.Wq3, E.K1,),
-        (E.Oy1, E.Od1,),
-        (),
+        (),
+        (E.Wq2, E.Sq, E.Oy1, E.Oy0, E.Wq3, E.K1,),
+        (E.Od1, E.Ox3,),
+        (),
+        (),
+        (E.Od0, E.Kp,),
         (E.Od2,),
-        (E.Od0, E.Kp,),
-        (),
         (E.Od3,),
         (),
         (),
         (),
     ),
     (0, 1): (
-        (E.On0, E.Ty, E.W0k, E.Tx, E.W0q, E.Sk, E.Sh0, E.Tp, E.TF, E.On1, E.Sq, E.On2, E.Wq1, E.Wk1, E.Sh1, E.Sh2,),
-        (E.Wk2, E.Ox2,),
-        (E.Wk3,),
-        (E.Oy2, E.Ox3, E.On3, E.Wq2, E.Sh3, E.Oy0,),
-        (E.K2,),
-        (),
-        (E.Ox1,),
-        (E.Od2, E.Wq3, E.Od3,),
-        (E.K1, E.Oy3,),
-        (),
-        (E.Oy1, E.Ox0, E.Od1, E.Kp, E.Od0,),
+        (E.W0k, E.W0q, E.Ty, E.On0, E.Tx, E.Sk, E.Sh0, E.Sq, E.Tp, E.TF, E.On1, E.On2, E.Wq1, E.Wk1, E.Sh2, E.Sh1, E.Wk2,),
+        (E.Wk3, E.Ox2, E.Oy2,),
+        (E.Ox3,),
+        (E.Wq2, E.On3, E.Sh3,),
+        (E.Oy0,),
+        (),
+        (E.Ox1, E.K2, E.Od3, E.Wq3, E.Oy3, E.Oy1,),
+        (),
+        (E.K1,),
+        (),
+        (E.Od2, E.Od0, E.Ox0, E.Od1, E.Kp,),
         (),
         (),
         (),
@@ -223,34 +223,34 @@
         (),
     ),
     (1, 0): (
-        (E.Ty, E.Tp, E.On0, E.W0k, E.TF, E.Tx, E.Wk1, E.On1, E.Sh0,),
-        (E.Wq3, E.Sk, E.Wk3, E.On2, E.Wq1, E.Sh2, E.W0q, E.Od3, E.Sh1, E.Ox0, E.Wk2, E.Od0, E.On3, E.Ox2,),
+        (E.Wq3, E.Ty, E.W0k, E.On0, E.TF, E.Wk1, E.On1, E.Tp, E.Tx, E.Sh0,),
+        (E.Sk, E.Wq1, E.On2, E.W0q, E.Ox0, E.Sh2, E.Sh1, E.Wk3, E.Wk2, E.Od3, E.Ox2,),
         (E.Oy1,),
-        (E.K1, E.Sq, E.Oy2, E.Wq2,),
-        (),
-        (E.Ox1,),
+        (E.On3, E.Od0, E.K1, E.Wq2, E.Sq,),
+        (E.Oy2, E.Ox1,),
+        (),
+        (),
         (E.Oy0,),
-        (),
         (E.Od2,),
-        (E.K2,),
-        (E.Kp, E.Od1, E.Ox3,),
+        (E.K2, E.Od1,),
+        (E.Kp,),
+        (),
         (),
         (E.Oy3,),
-        (),
-        (),
-        (E.Sh3,),
+        (E.Sh3, E.Ox3,),
+        (),
     ),
     (1, 1): (
-        (E.On0, E.Ty, E.W0k, E.W0q, E.Tx, E.Sk, E.Sh0, E.K2, E.Tp, E.On1, E.On3, E.TF, E.Sq, E.Sh1, E.Ox3, E.Wk1,),
-        (E.On2, E.Wk3, E.Ox0,),
-        (E.Wk2, E.Wq1, E.Sh2,),
+        (E.K2, E.Ty, E.W0k, E.W0q, E.On0, E.Tx, E.Sk, E.Sh0, E.Tp, E.Sq, E.On1, E.On3, E.TF, E.Sh1, E.Wk3, E.Wk1,),
+        (E.Ox3, E.On2, E.Wk2, E.Wq1, E.Ox0,),
+        (E.Sh2,),
         (E.Od0,),
-        (),
-        (),
-        (E.Ox1, E.Oy2, E.Wq2, E.K1, E.Oy3,),
-        (E.Kp, E.Oy0, E.Sh3, E.Oy1,),
-        (E.Wq3, E.Od1, E.Ox2, E.Od3,),
-        (),
+        (E.Wq3,),
+        (),
+        (E.Oy2, E.Ox1, E.Wq2, E.K1, E.Sh3, E.Oy3, E.Oy1,),
+        (E.Kp,),
+        (E.Oy0,),
+        (E.Od3, E.Od1, E.Ox2,),
         (),
         (E.Od2,),
         (),
@@ -259,15 +259,15 @@
         (),
     ),
     (2, 0): (
-        (E.Ty, E.Tp, E.W0k, E.W0q, E.On0, E.Sk, E.TF, E.Tx, E.Wk3, E.On1, E.Wk1, E.Od3, E.Ox0,),
-        (E.Sh0, E.On2, E.Sq, E.Wk2, E.Wq2,),
-        (),
-        (E.Sh2, E.Sh1,),
-        (E.Ox3, E.Ox2, E.Wq1, E.Ox1, E.Oy3, E.K2, E.Oy2, E.Od0, E.Oy0,),
+        (E.W0k, E.Ty, E.W0q, E.Tp, E.On0, E.TF, E.Tx, E.On1,),
+        (E.Sk, E.Ox0, E.Sh0, E.Wk1, E.Od3, E.On2, E.Wk2,),
+        (),
+        (E.Sq, E.Sh2,),
+        (E.Wq1, E.Wq3, E.Sh1, E.Wq2, E.Ox2, E.Oy3, E.Ox1, E.K2, E.Wk3, E.Od0, E.Ox3, E.Oy0, E.Oy2,),
         (E.Oy1,),
-        (E.Wq3, E.On3, E.K1, E.Od2, E.Od1,),
-        (),
-        (E.Sh3,),
+        (E.Od2, E.K1, E.On3, E.Sh3,),
+        (E.Od1,),
+        (),
         (),
         (E.Kp,),
         (),
@@ -277,35 +277,35 @@
         (),
     ),
     (2, 1): (
-        (E.Ty, E.On0, E.W0k, E.Sh0, E.W0q, E.On1, E.Tx, E.Sk, E.Tp, E.Sh1, E.Wk1, E.TF, E.Wk2, E.Sq,),
-        (E.Od3, E.Ox3, E.On3, E.On2,),
-        (E.Sh2,),
-        (E.Oy0,),
-        (),
-        (E.Wq1, E.Wq2, E.Wk3,),
-        (),
-        (E.Ox1,),
-        (),
-        (E.K1, E.Wq3, E.Ox2,),
-        (E.Sh3, E.Oy1, E.Oy2, E.Ox0, E.K2, E.Kp, E.Od1,),
-        (E.Oy3, E.Od0, E.Od2,),
+        (E.W0k, E.Ty, E.On0, E.Tp, E.Sh0, E.W0q, E.On1, E.Tx, E.Sh1, E.Sk, E.Wk1, E.TF, E.Wk2, E.Od3, E.Sq,),
+        (E.Wq3, E.Ox3, E.Oy0, E.On3,),
+        (E.Wk3, E.On2, E.Sh2, E.Wq1,),
+        (),
+        (E.Wq2,),
+        (),
+        (),
+        (),
+        (E.Ox1, E.K1,),
+        (E.Oy2, E.Oy1, E.Ox0, E.Ox2, E.Sh3, E.K2, E.Kp,),
+        (E.Od1, E.Oy3,),
+        (E.Od2, E.Od0,),
         (),
         (),
         (),
         (),
     ),
     (3, 0): (
-        (E.Ty, E.Tp, E.W0q, E.On0, E.W0k, E.On1, E.TF, E.On2, E.Sh0, E.Wk1, E.Wq1, E.Tx, E.Sk, E.Ox2, E.Ox0, E.Sh1, E.On3, E.Ox1, E.Sh2, E.Wk2, E.Od1,),
-        (E.Sh3, E.Wq2,),
-        (),
-        (E.Oy0, E.Sq, E.Wk3,),
-        (),
-        (E.Od2, E.Oy2,),
-        (E.Ox3, E.Oy3,),
-        (),
-        (E.Wq3,),
-        (E.K1, E.K2,),
-        (E.Oy1, E.Kp,),
+        (E.W0q, E.Ty, E.TF, E.On0, E.W0k, E.On1, E.Sh0, E.Ox0, E.Tp, E.On2, E.Wq1, E.Wk1, E.Sk, E.Tx, E.Ox2, E.Sh1, E.On3, E.Ox1, E.Wk2, E.Sh2,),
+        (E.Od1, E.Sh3,),
+        (),
+        (E.Wk3, E.Oy0, E.Wq2,),
+        (E.Sq, E.Oy2, E.Wq3,),
+        (),
+        (E.Oy3, E.Ox3, E.Od2,),
+        (E.Oy1,),
+        (),
+        (),
+        (E.K1, E.K2, E.Kp,),
         (E.Od3, E.Od0,),
         (),
         (),
@@ -313,19 +313,19 @@
         (),
     ),
     (3, 1): (
-        (E.Ty, E.W0k, E.On0, E.W0q, E.Tx, E.On1, E.Sh0, E.Sk, E.On2, E.Tp, E.TF, E.Sh2, E.Sq,),
-        (E.Sh1, E.Wk1, E.Ox0, E.Oy2, E.Wk3, E.On3,),
-        (E.Ox2,),
-        (E.Wk2, E.Sh3, E.Wq1, E.Od2,),
+        (E.On0, E.W0k, E.W0q, E.Tx, E.Ty, E.Sh0, E.Tp, E.Sk, E.On1, E.Sq, E.On2, E.Sh2, E.TF,),
+        (E.Wk3, E.Wk1, E.Sh1, E.Oy2, E.Ox0, E.On3,),
+        (E.Ox2, E.Wk2,),
+        (E.Sh3,),
+        (E.Oy1, E.Wq1,),
+        (E.K1, E.Wq3,),
         (E.Wq2,),
-        (E.Oy1, E.K1,),
-        (E.Ox1,),
-        (E.Ox3, E.Wq3,),
-        (),
-        (E.K2,),
-        (E.Od0, E.Oy3, E.Oy0, E.Kp,),
+        (),
+        (),
+        (E.K2, E.Ox1, E.Ox3,),
+        (E.Oy0, E.Oy3, E.Od0, E.Od2, E.Kp, E.Od3,),
         (E.Od1,),
-        (E.Od3,),
+        (),
         (),
         (),
         (),
@@ -879,27 +879,27 @@
             ATT[order[i]], WO[pl.ds(pl.multiple_of(order[i] * width + n * cut, 128), cut), :],
             (((1,), (1,)), ((), ())), preferred_element_type=F32,
         )
-        PR[n] = acc if i == 0 else PR[n] + acc
+        value = acc if i == 0 else PR[n] + acc
+        PR[n] = value
+        if i == heads - 1:
+            square = value * value
+            DEN[0:rows, :] += sum(square[:, k : k + HD] for k in range(0, cut, HD))
 
     order = (hg, 2 * (1 - y) + x, 2 * y + 1 - x, 2 * (1 - y) + 1 - x)
+    DEN[...] = jnp.zeros_like(DEN)
     for i in range(heads):
-        events(3 + 2 * LINE + i)
+        if i == heads - 1:
+            events(3 + 2 * LINE + i)
+            everyone(lambda moves: moves.emitted(LINE - 1))
+            for past in range(i):
+                around(LINE - 1, functools.partial(emit, past))
+        events(3 + 2 * LINE + i + i // (heads - 1))
         everyone(lambda moves: moves.gathered(i))
-        for k in range(LINE - 1):
+        for k in range(LINE - 1 + i // (heads - 1)):
             if i == 0:
                 everyone(lambda moves: moves.emitted(k))
             around(k, functools.partial(emit, i))
-    events(3 + 2 * LINE + heads)
-    everyone(lambda moves: moves.emitted(LINE - 1))
-
-    def emit_all(n):
-        for i in range(heads):
-            emit(i, n)
-
-    around(LINE - 1, emit_all)
-    squares = jnp.zeros((rows, 1), F32)
-    for h in range(heads):
-        squares += jnp.sum(PR[h] * PR[h], axis=1, keepdims=True)
+    squares = jnp.sum(DEN[0:rows, :], axis=1, keepdims=True)
     scale = lax.rsqrt(squares / width + EPS)
     kept = other.astype(jnp.int32)
 

time: 83.8 us -> 83.9 us (level)
  no operation moved by 1% of the time
where the time goes in v5:
time: 83.9 us; the launch traced here: 83.4 us
  Pallas kernels  82 us (98%)
  local copies, waits for them, and re-layouts  1.41 us (2%)
    pallas_call x1, Pallas kernels, fused(): pl.pallas_call(functools.partial(kernel, seq, heads, rows, width, most),...  82 us

profile of v5, /device:TPU:29, one launch (start us, length us, event | category | flops | bytes accessed | tf_op | source)
XLA Modules:
  0.0 83.4 jit_solution(9124940707857899408)
XLA Ops:
  0.0 82.0 %shard_map.91 = bf16[256,4608]{1,0:T(8,128)(2,1)S(1)} custom-call(bf16[256,1152]{1,0:T(8,128)(2,1)} %tok.1, s32[1,256]{1,0:T(1,128)} %bitcast.3, bf16[576,256]{1,0:T(8,128)(2,1)} %wq.1, bf16[576,128]{1,0:T(8,128)(2,1)} %wk.1, bf16[576,128]{1,0:T(8,128)(2,1)} %wv.1, bf16[576,256]{1,0:T(8,128)(2,1)} %bitcast.2, f32[4608]{0:T(1024)} %pre_in.1, f32[4608]{0:T(1024)} %post_in.1, ...), custom_call_target="tpu_custom_call" | custom-call | tf_op jit(solution)/shard_map/pallas_call | solution.py:929
  82.0 1.4 %copy.11 = bf16[256,4608]{1,0:T(8,128)(2,1)} copy(bf16[256,4608]{1,0:T(8,128)(2,1)S(1)} %shard_map.91) | data formatting | bytes 4718592
